TPU v7x, 256 devices: a whole 4x4x8 slice. The times are simulated.
256 devices in a mesh: gz: 8 (over z), xy: 32 (over x, y, core).
Axes of the slice: x: 4, y: 4, z: 8, core: 2. Of those that a mesh axis runs over, the one named last changes fastest.
Arguments:
- volume: float32 [128, 1536, 128], P('gz', 'xy'), may hold values from 0 to 1
- measured: float32 [2, 5, 160, 1536], P(None, None, 'gz', 'xy'), may hold values from 0 to 1
- view_order: int32 [48], replicated, may hold values from 0 to 47, each once
Outputs:
- volume_out: float32 [128, 1536, 128], P('gz', 'xy')
- residual: float32 [5, 160, 1536], P(None, 'gz', 'xy')
Inputs may be any that keep to these rules, and one draw needn't show every extreme that they name: `view_order`: A permutation of the numbers 0 to 47.
All inputs are finite; a program needn't handle non-finite values.
Results may differ from a plain program's by a relative error of at most 0.00078.
Values may be sent and summed in bfloat16 or wider, within the bound.
A program may use at most 64 MiB of HBM per device.

v0:
```python
import functools
import math

import jax
import jax.numpy as jnp
from jax import lax
from jax.experimental import pallas as pl
from jax.experimental.pallas import tpu as pltpu
from jax.sharding import PartitionSpec as P

Z_DEV = 16
X_DEV = 48
COLS_DEV = 48
NY = 128
VIEWS = 5
SUBSETS = 2
ANGLES = 48
ROWS_DEV = 20
HALF = X_DEV // 2
WIN = 48
GROUPS = 5
OWNERS = VIEWS * GROUPS
MESH = pl.DeviceIdType.MESH
HIGHEST = lax.Precision.HIGHEST
F32 = jnp.float32
BF16 = jnp.bfloat16


def iota(shape, dim):
    return lax.broadcasted_iota(jnp.int32, shape, dim)


def kernel(
    gz, xy, view_ref, vol_ref, meas_ref, out_ref, resid_ref,
    it, up, ws, shift, trig, weights, data, window, ones_window,
    send_m, recv_m, meas_rows, send_a, recv_a, send_t, recv_t,
    starts, total, total_t, res, send_c, recv_c, send_d, recv_d, turned,
    sem_vol, sem_ms, sem_mr, sem_as, sem_ar, sem_ah, sem_ts, sem_tr, sem_cs, sem_cr, sem_ch, sem_ds, sem_dr,
):
    g = lax.axis_index("gz")
    j = lax.axis_index("xy")
    nx_all, ny_all, dc_all = X_DEV * xy, NY, COLS_DEV * xy
    dr_all, nz_all = ROWS_DEV * gz, Z_DEV * gz
    owner = j < OWNERS
    own_view = lax.rem(lax.div(j, GROUPS), VIEWS)
    own_group = lax.rem(j, GROUPS)
    first_group = jnp.logical_and(owner, own_group == 0)
    last_group = jnp.logical_and(owner, own_group == GROUPS - 1)
    below, above = g > 0, g < gz - 1

    vol_copy = pltpu.make_async_copy(vol_ref, it, sem_vol)
    vol_copy.start()

    barrier = pltpu.get_barrier_semaphore()

    def greet(plane, device):
        pl.semaphore_signal(barrier, inc=1, device_id=(plane, device), device_id_type=MESH)

    def greet_plane(i, carry):
        @pl.when(i != j)
        def _():
            greet(g, i)

        @pl.when(jnp.logical_and(below, jnp.logical_or(first_group, jnp.logical_and(i < OWNERS, lax.rem(i, GROUPS) == GROUPS - 1))))
        def _():
            greet(g - 1, i)

        @pl.when(jnp.logical_and(above, jnp.logical_or(last_group, jnp.logical_and(i < OWNERS, lax.rem(i, GROUPS) == 0))))
        def _():
            greet(g + 1, i)

        return carry

    lax.fori_loop(0, xy, greet_plane, 0)
    greeted = (
        xy - 1
        + jnp.where(below, jnp.where(first_group, xy, VIEWS), 0)
        + jnp.where(above, jnp.where(last_group, xy, VIEWS), 0)
    )

    lane = iota((8, 128), 1)
    sub = iota((8, 128), 0)
    lane_f = lane.astype(F32)
    sub_f = sub.astype(F32)
    band = lane // 16
    source = 2.0 * nx_all
    scale = 0.9 * (dc_all / nx_all)
    middle = (dc_all - 1) / 2.0
    x_first = (j * X_DEV).astype(F32)

    def project(x, y, cosine, sine):
        along = x * cosine + y * sine
        depth = y * cosine - x * sine
        return middle + scale * along * source / (source + depth)

    def hat(row, slice_id):
        position = (dr_all - 1) / 2.0 + 0.96 * (dr_all / nz_all) * (slice_id - (nz_all - 1) / 2.0)
        return jnp.maximum(0.0, 1.0 - jnp.abs(position - row) / 2.0)

    def rounded(x):
        return x.astype(BF16).astype(F32)

    def geometry(s):
        for v in range(VIEWS):
            number = jnp.full((8, 128), view_ref[s * VIEWS + v], jnp.int32).astype(F32)
            angle = 2.0 * math.pi * number / ANGLES
            cosine, sine = jnp.cos(angle), jnp.sin(angle)
            trig[s, v, 0] = cosine
            trig[s, v, 1] = sine
            y_low = (band * 16).astype(F32) - (ny_all - 1) / 2.0
            base = []
            for h in range(2):
                x_low = (x_first + HALF * h) - (nx_all - 1) / 2.0
                corners = [
                    project(x, y, cosine, sine)
                    for x in (x_low, x_low + (HALF - 1))
                    for y in (y_low, y_low + 15.0)
                ]
                lowest = jnp.minimum(jnp.minimum(corners[0], corners[1]), jnp.minimum(corners[2], corners[3]))
                start = jnp.floor((lowest - 0.03125) * 0.125) * 8.0
                base.append(start)
                shift[s, v, h] = (start - 256.0 * jnp.floor(start * (1.0 / 256.0))).astype(jnp.int32)
            for block in range(X_DEV // 8):
                x = (x_first + (8.0 * block + sub_f)) - (nx_all - 1) / 2.0
                y = lane_f - (ny_all - 1) / 2.0
                u = project(x, y, cosine, sine)
                up[s, v, 8 * block : 8 * block + 8, :] = u - base[block // (HALF // 8)]
                low = jnp.floor(u)
                both = rounded(jnp.maximum(0.0, 1.0 - jnp.abs(u - low))) + rounded(
                    jnp.maximum(0.0, 1.0 - jnp.abs(u - (low + 1.0)))
                )
                rows = slice(8 * block, 8 * block + 8)
                ws[s, rows, :] = both if v == 0 else ws[s, rows, :] + both

    window_ids = iota((WIN, 128), 0).astype(F32)

    def make_weights(s):
        def one(x, carry):
            columns = pl.ds(pl.multiple_of(x * 128, 128), 128)
            for h in range(2):
                for v in range(VIEWS):
                    u = up[s, v, pl.ds(HALF * h + x, 1), :]
                    w = jnp.maximum(0.0, 1.0 - jnp.abs(u - window_ids))
                    weights[2 * s + h, v * WIN : (v + 1) * WIN, columns] = w.astype(BF16)
            return carry

        lax.fori_loop(0, HALF, one, 0)

    band_masks = [(iota((16, 128), 1) // 16 == q).astype(F32).astype(BF16) for q in range(8)]

    def spread(values, h, x):
        columns = pl.ds(pl.multiple_of(x * 128, 128), 128)
        values = values.astype(BF16)
        for q in range(8):
            data[h, 16 * q : 16 * q + 16, columns] = values * band_masks[q]

    row_local = (iota((56, 128), 0) // 8) * 4 + iota((56, 128), 0) % 4 - 4
    row_all = g * ROWS_DEV + row_local
    inside = jnp.logical_and(row_all >= 0, row_all < dr_all)
    slice_all = (g * Z_DEV + iota((56, 128), 1) % 16).astype(F32)
    row_hat = jnp.where(inside, hat(row_all.astype(F32), slice_all), 0.0)
    in_low = iota((56, 128), 0) % 8 < 4
    hat_low = jnp.where(in_low, row_hat, 0.0)
    hat_high = jnp.where(in_low, 0.0, row_hat)

    slices = (g * Z_DEV + iota((16, 128), 0)).astype(F32)
    slice_total = jnp.zeros((16, 1), F32)
    for part in range(-(-dr_all // 128)):
        rows = 128 * part + iota((16, 128), 1)
        weight = jnp.where(rows < dr_all, hat(rows.astype(F32), slices), 0.0)
        slice_total = slice_total + jnp.sum(weight, axis=1, keepdims=True)
    slice_total = jnp.broadcast_to(slice_total, (16, 128))
    own_row = (g * ROWS_DEV + own_group * 4 + sub % 4).astype(F32)
    ray_row = jnp.zeros((8, 1), F32)
    for part in range(-(-nz_all // 128)):
        ids = 128 * part + lane
        weight = jnp.where(ids < nz_all, hat(own_row, ids.astype(F32)), 0.0)
        ray_row = ray_row + jnp.sum(weight, axis=1, keepdims=True)
    ray_row = jnp.broadcast_to(ray_row, (8, 128))
    column_ids = [(256 * m + 128 * (sub // 4) + lane).astype(F32) for m in range(dc_all // 256)]

    def to_owners(src, dst, send_sem, recv_sem):
        def one(o, carry):
            @pl.when(o != j)
            def _():
                pltpu.make_async_remote_copy(
                    src_ref=src(o), dst_ref=dst, send_sem=send_sem, recv_sem=recv_sem,
                    device_id=(g, o), device_id_type=MESH,
                ).start()

            @pl.when(o == j)
            def _():
                pltpu.make_async_copy(src(o), dst, recv_sem).start()

            return carry

        lax.fori_loop(0, OWNERS, one, 0)

    def sent_to_owners(ref, sem):
        @pl.when(owner)
        def _():
            pltpu.make_async_copy(ref.at[0 : OWNERS - 1], ref.at[0 : OWNERS - 1], sem).wait()

        @pl.when(jnp.logical_not(owner))
        def _():
            pltpu.make_async_copy(ref.at[0:OWNERS], ref.at[0:OWNERS], sem).wait()

    def arrived(ref, sem):
        pltpu.make_async_copy(ref, ref, sem).wait()

    geometry(0)

    for v in range(VIEWS):
        for k in range(GROUPS):
            for s in range(SUBSETS):
                send_m[v * GROUPS + k, 4 * s : 4 * s + 4, 0:COLS_DEV] = meas_ref[s, v, 4 * k : 4 * k + 4, :]
    turn = lax.rem(j * COLS_DEV, 128)
    for o in range(OWNERS):
        send_m[o] = pltpu.roll(send_m[o], turn, 1)

    make_weights(0)

    def fill_ones(x, carry):
        columns = pl.ds(pl.multiple_of(x * 128, 128), 128)
        for h in range(2):
            for q in range(8):
                first = iota((16, 128), 0) == 0
                row = jnp.where(jnp.logical_and(first, iota((16, 128), 1) // 16 == q), 1.0, 0.0)
                data[h, 128 + 16 * q : 128 + 16 * q + 16, columns] = row.astype(BF16)
        return carry

    lax.fori_loop(0, HALF, fill_ones, 0)
    vol_copy.wait()

    def fill_data(x, carry):
        for h in range(2):
            spread(it[pl.ds(HALF * h + x, 16, stride=X_DEV), :], h, x)
        return carry

    lax.fori_loop(0, HALF, fill_data, 0)

    pl.semaphore_wait(barrier, greeted)
    to_owners(lambda o: send_m.at[o], recv_m.at[j], sem_ms, sem_mr)

    def forward(s):
        for h in range(2):
            sums = lax.dot_general(
                weights[2 * s + h], data[h], (((1,), (1,)), ((), ())), preferred_element_type=F32
            )
            for v in range(VIEWS):
                offset = shift[s, v, h]
                for part, target in ((0, window), (1, ones_window)):
                    rows = [
                        sums[v * WIN + 8 * i : v * WIN + 8 * i + 8, 128 * part : 128 * part + 128]
                        for i in range(WIN // 8)
                    ] + [None] * (32 - WIN // 8)
                    for bit in (8, 16, 32, 64, 128):
                        moved = (offset & bit) != 0
                        step = bit // 8
                        new = []
                        for i in range(32):
                            old, other = rows[i], rows[(i - step) % 32]
                            if old is None and other is None:
                                new.append(None)
                            elif old is None:
                                new.append(jnp.where(moved, other, 0.0))
                            elif other is None:
                                new.append(jnp.where(moved, 0.0, old))
                            else:
                                new.append(jnp.where(moved, other, old))
                        rows = new
                    for i in range(32):
                        at = slice(256 * v + 8 * i, 256 * v + 8 * i + 8)
                        target[at, :] = rows[i] if h == 0 else target[at, :] + rows[i]
        for v in range(VIEWS):
            totals = lax.dot_general(
                jnp.ones((8, 128), F32), ones_window[256 * v : 256 * v + 256, :],
                (((1,), (1,)), ((), ())), precision=HIGHEST, preferred_element_type=F32,
            )
            message = jnp.where(sub < 4, totals[:, 0:128], totals[:, 128:256])
            low = lax.dot_general(
                hat_low, window[256 * v : 256 * v + 128, :],
                (((1,), (1,)), ((), ())), precision=HIGHEST, preferred_element_type=F32,
            )
            high = lax.dot_general(
                hat_high, window[256 * v + 128 : 256 * v + 256, :],
                (((1,), (1,)), ((), ())), precision=HIGHEST, preferred_element_type=F32,
            )
            rows = low + high
            send_t[s, v] = message
            for k in range(GROUPS + 2):
                send_a[s, k, v] = rows[8 * k : 8 * k + 8, :]
        to_owners(
            lambda o: send_a.at[s, 1 + lax.rem(o, GROUPS), lax.div(o, GROUPS)],
            recv_a.at[s, 0, j], sem_as.at[s], sem_ar.at[s],
        )
        to_owners(lambda o: send_t.at[s, lax.div(o, GROUPS)], recv_t.at[s, j], sem_ts.at[s], sem_tr.at[s])

        def beside(v, carry):
            for there, plane, slot, device in (
                (below, g - 1, 0, GROUPS * v + GROUPS - 1),
                (above, g + 1, GROUPS + 1, GROUPS * v),
            ):
                @pl.when(there)
                def _():
                    pltpu.make_async_remote_copy(
                        src_ref=send_a.at[s, slot, v], dst_ref=recv_a.at[s, 1, j],
                        send_sem=sem_as.at[2 + s], recv_sem=sem_ah.at[s],
                        device_id=(plane, device), device_id_type=MESH,
                    ).start()

            return carry

        lax.fori_loop(0, VIEWS, beside, 0)

    has_beside = jnp.logical_or(jnp.logical_and(first_group, below), jnp.logical_and(last_group, above))

    def prepare_owner():
        arrived(recv_m, sem_mr)
        for block in range(dc_all // 128):
            first, last = 128 * block, 128 * block + 128
            value = jnp.zeros((8, 128), F32)
            for i in range(first // COLS_DEV, min(xy, -(-last // COLS_DEV))):
                low, high = max(COLS_DEV * i, first) - first, min(COLS_DEV * (i + 1), last) - first
                value = jnp.where(jnp.logical_and(lane >= low, lane < high), recv_m[i], value)
            at = 4 * (block % 2)
            for s in range(SUBSETS):
                meas_rows[s, block // 2, at : at + 4, :] = value[4 * s : 4 * s + 4, :]

    def window_starts(s):
        cosine, sine = trig[s, own_view, 0], trig[s, own_view, 1]

        def one(i, carry):
            x = jnp.full((8, 128), i * X_DEV, jnp.int32).astype(F32) + ((X_DEV - 1) / 2.0 - (nx_all - 1) / 2.0)
            starts[i] = jnp.floor(project(x, 0.0, cosine, sine)) - 128.0
            return carry

        lax.fori_loop(0, xy, one, 0)

    blocks = dc_all // 256

    def owner_work(s):
        arrived(recv_a.at[s, 0], sem_ar.at[s])
        arrived(recv_t.at[s], sem_tr.at[s])
        zero = tuple(jnp.zeros((8, 128), F32) for _ in range(2 * blocks))

        def add(i, sums):
            start = starts[i]
            message, column = recv_a[s, 0, i], recv_t[s, i]
            new = list(sums)
            for m in range(blocks):
                away = column_ids[m] - start
                hit = jnp.logical_and(away >= 0.0, away < 256.0)
                new[m] = new[m] + jnp.where(hit, message, 0.0)
                new[blocks + m] = new[blocks + m] + jnp.where(hit, column, 0.0)
            return tuple(new)

        sums = lax.fori_loop(0, xy, add, zero)
        for m in range(blocks):
            total[m] = sums[m]
            total_t[m] = sums[blocks + m]

        @pl.when(has_beside)
        def _():
            arrived(recv_a.at[s, 1], sem_ah.at[s])

            def add_beside(i, sums):
                start = starts[i]
                message = recv_a[s, 1, i]
                new = []
                for m in range(blocks):
                    away = column_ids[m] - start
                    hit = jnp.logical_and(away >= 0.0, away < 256.0)
                    new.append(sums[m] + jnp.where(hit, message, 0.0))
                return tuple(new)

            sums = lax.fori_loop(0, xy, add_beside, zero[:blocks])
            for m in range(blocks):
                total[m] = total[m] + sums[m]

        residuals = []
        for m in range(blocks):
            residual = meas_rows[s, m] - total[m] / jnp.maximum(ray_row * total_t[m], 1.0)
            res[m] = residual
            residuals.append(rounded(residual))

        def give(i, carry):
            start = starts[i]
            message = residuals[blocks - 1]
            for m in range(blocks - 2, -1, -1):
                message = jnp.where(column_ids[m] >= start, residuals[m], message)
            send_c[s, i] = message
            return carry

        lax.fori_loop(0, xy, give, 0)

        def send(i, carry):
            slot = recv_c.at[s, 1 + own_group, own_view]

            @pl.when(i != j)
            def _():
                pltpu.make_async_remote_copy(
                    src_ref=send_c.at[s, i], dst_ref=slot, send_sem=sem_cs.at[s], recv_sem=sem_cr.at[s],
                    device_id=(g, i), device_id_type=MESH,
                ).start()

            @pl.when(i == j)
            def _():
                pltpu.make_async_copy(send_c.at[s, i], slot, sem_cr.at[s]).start()

            @pl.when(jnp.logical_and(first_group, below))
            def _():
                pltpu.make_async_remote_copy(
                    src_ref=send_c.at[s, i], dst_ref=recv_c.at[s, GROUPS + 1, own_view],
                    send_sem=sem_cs.at[2 + s], recv_sem=sem_ch.at[s, 1],
                    device_id=(g - 1, i), device_id_type=MESH,
                ).start()

            @pl.when(jnp.logical_and(last_group, above))
            def _():
                pltpu.make_async_remote_copy(
                    src_ref=send_c.at[s, i], dst_ref=recv_c.at[s, 0, own_view],
                    send_sem=sem_cs.at[2 + s], recv_sem=sem_ch.at[s, 0],
                    device_id=(g + 1, i), device_id_type=MESH,
                ).start()

            return carry

        lax.fori_loop(0, xy, send, 0)

    def owner_give_residual():
        residuals = [res[m] for m in range(blocks)]

        def give(i, carry):
            start = jnp.full((8, 128), i * COLS_DEV, jnp.int32).astype(F32)
            message = residuals[blocks - 1]
            for m in range(blocks - 2, -1, -1):
                message = jnp.where(column_ids[m] >= start, residuals[m], message)
            send_d[i] = message
            return carry

        lax.fori_loop(0, xy, give, 0)

        def send(i, carry):
            @pl.when(i != j)
            def _():
                pltpu.make_async_remote_copy(
                    src_ref=send_d.at[i], dst_ref=recv_d.at[j], send_sem=sem_ds, recv_sem=sem_dr,
                    device_id=(g, i), device_id_type=MESH,
                ).start()

            @pl.when(i == j)
            def _():
                pltpu.make_async_copy(send_d.at[i], recv_d.at[j], sem_dr).start()

            return carry

        lax.fori_loop(0, xy, send, 0)

    def backward(s):
        @pl.when(jnp.logical_not(below))
        def _():
            recv_c[s, 0] = jnp.zeros((VIEWS, 8, 128), F32)

        @pl.when(jnp.logical_not(above))
        def _():
            recv_c[s, GROUPS + 1] = jnp.zeros((VIEWS, 8, 128), F32)

        arrived(recv_c.at[s, 1 : GROUPS + 1], sem_cr.at[s])

        @pl.when(below)
        def _():
            arrived(recv_c.at[s, 0], sem_ch.at[s, 0])

        @pl.when(above)
        def _():
            arrived(recv_c.at[s, GROUPS + 1], sem_ch.at[s, 1])

        hats = jnp.concatenate([hat_low, hat_high], axis=1)
        for v in range(VIEWS):
            rows = jnp.concatenate([recv_c[s, k, v] for k in range(GROUPS + 2)], axis=0)
            smeared = rounded(
                lax.dot_general(
                    rows, hats, (((0,), (0,)), ((), ())), precision=HIGHEST, preferred_element_type=F32
                )
            )
            whole = [smeared[8 * i : 8 * i + 8, 128 * p : 128 * p + 128] for p in range(2) for i in range(16)]
            for h in range(2):
                offset = shift[s, v, h]
                now = whole
                for bit in (128, 64, 32, 16, 8):
                    step = bit // 8
                    moved = (offset & bit) != 0
                    now = [
                        jnp.where(moved, now[(i + step) % 32], now[i]) for i in range(WIN // 8 + step - 1)
                    ]
                for i in range(WIN // 8):
                    turned[h, v * WIN + 8 * i : v * WIN + 8 * i + 8, :] = now[i]
        sides = [jnp.transpose(turned[h]).astype(BF16) for h in range(2)]
        last = s == SUBSETS - 1

        def one(pair, carry):
            for h in range(2):
                columns = pl.ds(pl.multiple_of(pair * 256, 256), 256)
                back = lax.dot_general(
                    sides[h], weights[2 * s + h, :, columns], (((1,), (0,)), ((), ())),
                    preferred_element_type=F32,
                )
                for part in range(2):
                    x = 2 * pair + part
                    mine = back[112:128, 128 * part : 128 * part + 128]
                    for q in range(6, -1, -1):
                        mine = jnp.where(
                            jnp.concatenate([band, band], axis=0) == q,
                            back[16 * q : 16 * q + 16, 128 * part : 128 * part + 128], mine,
                        )
                    norm = slice_total * ws[s, pl.ds(HALF * h + x, 1), :]
                    at = pl.ds(HALF * h + x, 16, stride=X_DEV)
                    new = it[at, :] + mine / jnp.maximum(norm, 1.0)
                    if last:
                        out_ref[at, :] = new
                    else:
                        it[at, :] = new
                        spread(new, h, x)
            return carry

        lax.fori_loop(0, HALF // 2, one, 0)

    forward(0)

    @pl.when(owner)
    def _():
        prepare_owner()
        window_starts(0)
        owner_work(0)

    geometry(1)
    make_weights(1)
    backward(0)
    forward(1)

    @pl.when(owner)
    def _():
        window_starts(1)
        owner_work(1)
        owner_give_residual()

    backward(1)

    arrived(recv_d, sem_dr)
    begin = j * COLS_DEV
    turn_back = lax.rem(128 - lax.rem(begin, 128), 128)
    odd = lax.rem(lax.div(begin, 128), 2) == 1
    keep = lane < 128 - lax.rem(begin, 128)
    from_low = jnp.logical_xor(keep, odd)
    for v in range(VIEWS):
        for k in range(GROUPS):
            message = pltpu.roll(recv_d[v * GROUPS + k], turn_back, 1)
            other = pltpu.roll(message, 4, 0)
            value = jnp.where(from_low, message, other)
            resid_ref[v, 4 * k : 4 * k + 4, :] = value[0:4, 0:COLS_DEV]

    sent_to_owners(send_m, sem_ms)
    for s in range(SUBSETS):
        flat = recv_a.at[s, 0]
        sent_to_owners(flat, sem_as.at[s])
        sent_to_owners(flat, sem_ts.at[s])

        @pl.when(below)
        def _():
            arrived(send_a.at[s, 0], sem_as.at[2 + s])

        @pl.when(above)
        def _():
            arrived(send_a.at[s, GROUPS + 1], sem_as.at[2 + s])

        @pl.when(owner)
        def _():
            arrived(send_c.at[s, 0 : xy - 1], sem_cs.at[s])

            @pl.when(has_beside)
            def _():
                arrived(send_c.at[s], sem_cs.at[2 + s])

    @pl.when(owner)
    def _():
        arrived(send_d.at[0 : xy - 1], sem_ds)


def local(gz, xy, volume, measured, view_order):
    blocks = COLS_DEV * xy // 256
    dma = pltpu.SemaphoreType.DMA
    vmem = pltpu.VMEM
    out, resid = pl.pallas_call(
        functools.partial(kernel, gz, xy),
        out_shape=(
            jax.ShapeDtypeStruct((Z_DEV * X_DEV, NY), F32),
            jax.ShapeDtypeStruct((VIEWS, ROWS_DEV, COLS_DEV), F32),
        ),
        in_specs=[
            pl.BlockSpec(memory_space=pltpu.SMEM),
            pl.BlockSpec(memory_space=pl.ANY),
            pl.BlockSpec(memory_space=pltpu.VMEM),
        ],
        out_specs=(pl.BlockSpec(memory_space=pltpu.VMEM), pl.BlockSpec(memory_space=pltpu.VMEM)),
        scratch_shapes=[
            vmem((Z_DEV * X_DEV, NY), F32),
            vmem((SUBSETS, VIEWS, X_DEV, NY), F32),
            vmem((SUBSETS, X_DEV, NY), F32),
            vmem((SUBSETS, VIEWS, 2, 8, 128), jnp.int32),
            vmem((SUBSETS, VIEWS, 2, 8, 128), F32),
            vmem((2 * SUBSETS, VIEWS * WIN, HALF * NY), BF16),
            vmem((2, 256, HALF * NY), BF16),
            vmem((VIEWS * 256, 128), F32),
            vmem((VIEWS * 256, 128), F32),
            vmem((OWNERS, 8, 128), F32),
            vmem((xy, 8, 128), F32),
            vmem((SUBSETS, blocks, 8, 128), F32),
            vmem((SUBSETS, GROUPS + 2, VIEWS, 8, 128), F32),
            vmem((SUBSETS, 2, xy, 8, 128), F32),
            vmem((SUBSETS, VIEWS, 8, 128), F32),
            vmem((SUBSETS, xy, 8, 128), F32),
            vmem((xy, 8, 128), F32),
            vmem((blocks, 8, 128), F32),
            vmem((blocks, 8, 128), F32),
            vmem((blocks, 8, 128), F32),
            vmem((SUBSETS, xy, 8, 128), F32),
            vmem((SUBSETS, GROUPS + 2, VIEWS, 8, 128), F32),
            vmem((xy, 8, 128), F32),
            vmem((OWNERS, 8, 128), F32),
            vmem((2, VIEWS * WIN, 128), F32),
            dma(()), dma(()), dma(()), dma((4,)), dma((2,)), dma((2,)), dma((2,)), dma((2,)),
            dma((4,)), dma((2,)), dma((2, 2)), dma(()), dma(()),
        ],
        compiler_params=pltpu.CompilerParams(collective_id=0, has_side_effects=True),
    )(view_order, volume.reshape(Z_DEV * X_DEV, NY), measured)
    return out.reshape(Z_DEV, X_DEV, NY), resid


def solution(mesh):
    in_specs = (P("gz", "xy", None), P(None, None, "gz", "xy"), P())
    out_specs = (P("gz", "xy", None), P(None, "gz", "xy"))
    body = functools.partial(local, mesh.shape["gz"], mesh.shape["xy"])
    return jax.shard_map(body, mesh=mesh, in_specs=in_specs, out_specs=out_specs, check_vma=False)
```

profile of v0, /device:TPU:33, one launch (start us, length us, event | category | flops | bytes accessed | tf_op | source)
XLA Modules:
  0.0 56.6 jit_solution(17740786850293765931)
XLA Ops:
  0.6 1.6 %copy.5.meas_ref = f32[2,5,20,48]{3,2,1,0:T(8,128)} copy(f32[2,5,20,48]{3,0,2,1:T(2,128)} %param.4) | data formatting | bytes 76800 | tf_op args[1]
  2.2 52.0 %shard_map.50 = (f32[768,128]{1,0:T(8,128)}, f32[5,20,48]{2,1,0:T(8,128)}) custom-call(s32[48]{0:T(128)} %view_ref.1, f32[768,128]{1,0:T(8,128)} %bitcast.2, f32[2,5,20,48]{3,2,1,0:T(8,128)} %copy.5.meas_ref), custom_call_target="tpu_custom_call" | custom-call | tf_op jit(solution)/shard_map/pallas_call | solution.py:594
  54.2 0.0 copy-start
  54.2 1.8 %copy.8 = f32[16,48,128]{2,1,0:T(8,128)} copy(f32[16,48,128]{2,1,0:T(8,128)} %bitcast.3) | data formatting | bytes 786432
  56.0 0.0 copy-done
  56.0 0.6 %copy.9 = f32[5,20,48]{2,1,0:T(8,128)} copy(f32[5,20,48]{2,1,0:T(8,128)S(1)} %copy-done) | data formatting | bytes 38400
Async XLA Ops:
  54.2 1.8 %copy-start = (f32[5,20,48]{2,1,0:T(8,128)S(1)}, f32[5,20,48]{2,1,0:T(8,128)}, u32[]{:S(2)}) copy-start(f32[5,20,48]{2,1,0:T(8,128)} %get-tuple-element.9) | copy-start | bytes 57604
where the time goes:
time: 56.8 us; the launch traced here: 56.6 us
  Pallas kernels  52 us (92%)
  local copies, waits for them, and re-layouts  3.97 us (7%)
  between operations  0.65 us (1%)
    pallas_call x1, Pallas kernels, local(): pl.pallas_call(functools.partial(kernel, gz, xy), out_shape=(jax.ShapeDty...  52 us
    unnamed x5, local copies, waits for them, and re-layouts  3.97 us

commit v1 on v0

v1 whole, which is shorter than its diff:
```python
import functools
import math

import jax
import jax.numpy as jnp
from jax import lax
from jax.experimental import pallas as pl
from jax.experimental.pallas import tpu as pltpu
from jax.sharding import PartitionSpec as P

Z_DEV = 16
X_DEV = 48
COLS_DEV = 48
NY = 128
VIEWS = 5
SUBSETS = 2
ANGLES = 48
ROWS_DEV = 20
HALF = X_DEV // 2
WIN = 48
GROUPS = 3
SLOTS = 7
SIZES = (7, 7, 6)
OWNERS = VIEWS * GROUPS
MESSAGES = ((-1, GROUPS - 1), (0, 0), (0, 1), (0, 2), (1, 0))
KINDS = len(MESSAGES)
MESH = pl.DeviceIdType.MESH
F32 = jnp.float32
BF16 = jnp.bfloat16


def iota(shape, dim):
    return lax.broadcasted_iota(jnp.int32, shape, dim)


def kernel(
    gz, xy, view_hbm, vol_ref, meas_hbm, out_ref, resid_ref,
    views, it, meas, up, ws, shift, trig, weights, data, window, mixer, smearer,
    send_m, recv_m, meas_rows, send_a, recv_a, starts, total, send_c, recv_c, send_d, recv_d, turned,
    sem_view, sem_vol, sem_meas, sem_ms, sem_mr, sem_as, sem_ar, sem_ah, sem_cs, sem_cr, sem_ch, sem_ds, sem_dr,
):
    g = lax.axis_index("gz")
    j = lax.axis_index("xy")
    nx_all, ny_all, dc_all = X_DEV * xy, NY, COLS_DEV * xy
    dr_all, nz_all = ROWS_DEV * gz, Z_DEV * gz
    blocks = dc_all // 128
    chip = lax.div(j, 2)
    owner = jnp.logical_and(lax.rem(j, 2) == 1, chip < OWNERS)
    own_view = lax.rem(lax.div(chip, GROUPS), VIEWS)
    own_group = lax.rem(chip, GROUPS)
    first_group = jnp.logical_and(owner, own_group == 0)
    last_group = jnp.logical_and(owner, own_group == GROUPS - 1)
    below, above = g > 0, g < gz - 1
    give_down = jnp.logical_and(first_group, below)
    give_up = jnp.logical_and(last_group, above)
    has_beside = jnp.logical_or(give_down, give_up)

    view_copy = pltpu.make_async_copy(view_hbm, views, sem_view)
    vol_copy = pltpu.make_async_copy(vol_ref, it, sem_vol)
    meas_copy = pltpu.make_async_copy(meas_hbm, meas, sem_meas)
    view_copy.start()
    vol_copy.start()
    meas_copy.start()

    barrier = pltpu.get_barrier_semaphore()

    def greet(plane, device):
        pl.semaphore_signal(barrier, inc=1, device_id=(plane, device), device_id_type=MESH)

    def greet_all(plane):
        for i in range(xy):
            greet(plane, i)

    def next_owner(t):
        return 2 * lax.rem(chip + t, OWNERS) + 1

    def next_device(t):
        return lax.rem(j + t, xy)

    with jax.named_scope("greet"):
        @pl.when(owner)
        def _():
            for t in range(1, xy):
                greet(g, next_device(t))

        @pl.when(jnp.logical_not(owner))
        def _():
            for t in range(OWNERS):
                greet(g, next_owner(t))

        @pl.when(give_down)
        def _():
            greet_all(g - 1)

        @pl.when(jnp.logical_and(below, jnp.logical_not(first_group)))
        def _():
            for v in range(VIEWS):
                greet(g - 1, 2 * (GROUPS * v + GROUPS - 1) + 1)

        @pl.when(give_up)
        def _():
            greet_all(g + 1)

        @pl.when(jnp.logical_and(above, jnp.logical_not(last_group)))
        def _():
            for v in range(VIEWS):
                greet(g + 1, 2 * GROUPS * v + 1)

    greeted = (
        jnp.where(owner, xy - 1, OWNERS)
        + jnp.where(below, jnp.where(first_group, xy, VIEWS), 0)
        + jnp.where(above, jnp.where(last_group, xy, VIEWS), 0)
    )

    lane = iota((8, 128), 1)
    sub = iota((8, 128), 0)
    lane_f = lane.astype(F32)
    sub_f = sub.astype(F32)
    band = lane // 16
    source = 2.0 * nx_all
    scale = 0.9 * (dc_all / nx_all)
    middle = (dc_all - 1) / 2.0
    x_first = (j * X_DEV).astype(F32)

    def project(x, y, cosine, sine):
        along = x * cosine + y * sine
        depth = y * cosine - x * sine
        return middle + scale * along * source / (source + depth)

    def hat(row, slice_id):
        position = (dr_all - 1) / 2.0 + 0.96 * (dr_all / nz_all) * (slice_id - (nz_all - 1) / 2.0)
        return jnp.maximum(0.0, 1.0 - jnp.abs(position - row) / 2.0)

    def rounded(x):
        return x.astype(BF16).astype(F32)

    def in_two(x):
        high = rounded(x)
        return high, x - high

    def geometry(s):
        for v in range(VIEWS):
            number = jnp.full((8, 128), views[s * VIEWS + v], jnp.int32).astype(F32)
            angle = 2.0 * math.pi * number / ANGLES
            cosine, sine = jnp.cos(angle), jnp.sin(angle)
            trig[s, v, 0] = cosine
            trig[s, v, 1] = sine
            y_low = (band * 16).astype(F32) - (ny_all - 1) / 2.0
            base = []
            for h in range(2):
                x_low = (x_first + HALF * h) - (nx_all - 1) / 2.0
                corners = [
                    project(x, y, cosine, sine)
                    for x in (x_low, x_low + (HALF - 1))
                    for y in (y_low, y_low + 15.0)
                ]
                lowest = jnp.minimum(jnp.minimum(corners[0], corners[1]), jnp.minimum(corners[2], corners[3]))
                start = jnp.floor((lowest - 0.03125) * 0.125) * 8.0
                base.append(start)
                shift[s, v, h] = (start - 256.0 * jnp.floor(start * (1.0 / 256.0))).astype(jnp.int32)
            for block in range(X_DEV // 8):
                x = (x_first + (8.0 * block + sub_f)) - (nx_all - 1) / 2.0
                y = lane_f - (ny_all - 1) / 2.0
                u = project(x, y, cosine, sine)
                up[s, v, 8 * block : 8 * block + 8, :] = u - base[block // (HALF // 8)]
                low = jnp.floor(u)
                both = rounded(jnp.maximum(0.0, 1.0 - jnp.abs(u - low))) + rounded(
                    jnp.maximum(0.0, 1.0 - jnp.abs(u - (low + 1.0)))
                )
                rows = slice(8 * block, 8 * block + 8)
                ws[s, rows, :] = both if v == 0 else ws[s, rows, :] + both

    window_ids = iota((WIN, 128), 0).astype(F32)

    def make_weights(s):
        def one(x, carry):
            columns = pl.ds(pl.multiple_of(x * 128, 128), 128)
            for h in range(2):
                for v in range(VIEWS):
                    u = up[s, v, pl.ds(HALF * h + x, 1), :]
                    w = jnp.maximum(0.0, 1.0 - jnp.abs(u - window_ids))
                    weights[2 * s + h, v * WIN : (v + 1) * WIN, columns] = w.astype(BF16)
            return carry

        lax.fori_loop(0, HALF, one, 0)

    band_masks = [(iota((16, 128), 1) // 16 == q).astype(F32).astype(BF16) for q in range(8)]

    def spread(values, h, x):
        columns = pl.ds(pl.multiple_of(x * 128, 128), 128)
        values = values.astype(BF16)
        for q in range(8):
            data[h, 16 * q : 16 * q + 16, columns] = values * band_masks[q]

    def row_tables():
        shape = (128, 128)
        at = iota(shape, 0)
        kind, half, slot = at // 16, (at // 8) % 2, at % 8
        row = jnp.where(kind == 0, slot + (SLOTS * MESSAGES[0][1] - ROWS_DEV), SLOTS * (kind - 1) + slot)
        row = jnp.where(kind == KINDS - 1, slot + ROWS_DEV, row)
        size = jnp.where(jnp.logical_or(kind == 0, kind == GROUPS), SIZES[-1], SLOTS)
        row_all = g * ROWS_DEV + row
        inside = jnp.logical_and(jnp.logical_and(row_all >= 0, row_all < dr_all), slot < size)
        inside = jnp.logical_and(inside, kind < KINDS)
        slice_all = (g * Z_DEV + iota(shape, 1) % 16).astype(F32)
        row_hat = jnp.where(inside, hat(row_all.astype(F32), slice_all), 0.0)
        own = jnp.logical_and(jnp.logical_and(kind >= 1, kind <= GROUPS), slot == 7)
        counts = jnp.where(jnp.logical_and(own, iota(shape, 1) % 16 < 2), 1.0, 0.0)
        count = 16 * KINDS
        for b in range(2):
            mine = half == b
            high, low = in_two(jnp.where(mine, row_hat, 0.0))
            ones = jnp.where(mine, counts, 0.0)
            smearer[0:128, 128 * b : 128 * b + 128] = high.astype(BF16)
            smearer[128:256, 128 * b : 128 * b + 128] = low.astype(BF16)
            for part, first, second in ((0, high, low), (1, high, low), (2, ones, jnp.zeros(shape, F32))):
                columns = slice(384 * b + 128 * part, 384 * b + 128 * part + 128)
                mixer[0:count, columns] = first[0:count].astype(BF16)
                mixer[count : 2 * count, columns] = second[0:count].astype(BF16)

    slices = (g * Z_DEV + iota((16, 128), 0)).astype(F32)
    slice_total = jnp.zeros((16, 1), F32)
    for part in range(-(-dr_all // 128)):
        rows = 128 * part + iota((16, 128), 1)
        weight = jnp.where(rows < dr_all, hat(rows.astype(F32), slices), 0.0)
        slice_total = slice_total + jnp.sum(weight, axis=1, keepdims=True)
    slice_total = jnp.broadcast_to(slice_total, (16, 128))
    own_row = (g * ROWS_DEV + own_group * SLOTS + sub).astype(F32)
    ray_row = jnp.zeros((8, 1), F32)
    for part in range(-(-nz_all // 128)):
        ids = 128 * part + lane
        weight = jnp.where(ids < nz_all, hat(own_row, ids.astype(F32)), 0.0)
        ray_row = ray_row + jnp.sum(weight, axis=1, keepdims=True)
    ray_row = jnp.broadcast_to(ray_row, (8, 128))
    own_slot = sub < jnp.where(own_group == GROUPS - 1, SIZES[-1], SLOTS)
    column_ids = [(128 * m + lane).astype(F32) for m in range(blocks)]

    def remote(src, dst, send_sem, recv_sem, plane, device):
        pltpu.make_async_remote_copy(
            src_ref=src, dst_ref=dst, send_sem=send_sem, recv_sem=recv_sem,
            device_id=(plane, device), device_id_type=MESH,
        ).start()

    def arrived(ref, sem):
        pltpu.make_async_copy(ref, ref, sem).wait()

    def to_owners(src, dst, send_sem, recv_sem):
        for t in range(1, OWNERS):
            device = next_owner(t)
            remote(src(lax.div(device, 2)), dst, send_sem, recv_sem, g, device)

        @pl.when(jnp.logical_not(owner))
        def _():
            device = next_owner(0)
            remote(src(lax.div(device, 2)), dst, send_sem, recv_sem, g, device)

    def with_owners(ref, sem):
        @pl.when(owner)
        def _():
            arrived(ref.at[0 : OWNERS - 1], sem)

        @pl.when(jnp.logical_not(owner))
        def _():
            arrived(ref.at[0:OWNERS], sem)

    def table(x, carry):
        columns = pl.ds(pl.multiple_of(x * 128, 128), 128)
        for h in range(2):
            for q in range(8):
                pair = iota((16, 128), 0) < 2
                row = jnp.where(jnp.logical_and(pair, iota((16, 128), 1) // 16 == q), 1.0, 0.0)
                data[h, 128 + 16 * q : 128 + 16 * q + 16, columns] = row.astype(BF16)
        return carry

    def fill_data(x, carry):
        for h in range(2):
            spread(it[pl.ds(HALF * h + x, 16, stride=X_DEV), :], h, x)
        return carry

    view_copy.wait()
    with jax.named_scope("geom0"):
        geometry(0)
    with jax.named_scope("mw0"):
        make_weights(0)
    with jax.named_scope("tables"):
        row_tables()
        lax.fori_loop(0, HALF, table, 0)
    with jax.named_scope("fill"):
        vol_copy.wait()
        lax.fori_loop(0, HALF, fill_data, 0)

    with jax.named_scope("measured"):
        meas_copy.wait()
        turn = lax.rem(j * COLS_DEV, 128)
        for v in range(VIEWS):
            for k in range(GROUPS):
                o = GROUPS * v + k
                send_m[o] = jnp.zeros((16, 128), F32)
                for s in range(SUBSETS):
                    for slot in range(SIZES[k]):
                        send_m[o, 8 * s + slot, 0:COLS_DEV] = meas[v, SLOTS * k + slot, s, :]
        for o in range(OWNERS):
            send_m[o] = pltpu.roll(send_m[o], turn, 1)

    with jax.named_scope("barrier"):
        pl.semaphore_wait(barrier, greeted)

    def send_measured():
        to_owners(lambda o: send_m.at[o], recv_m.at[j], sem_ms, sem_mr)

        @pl.when(owner)
        def _():
            recv_m[j] = send_m[chip]

    def forward(s):
        with jax.named_scope("f_dot"):
            sums = [
                lax.dot_general(
                    weights[2 * s + h], data[h], (((1,), (1,)), ((), ())), preferred_element_type=F32
                )
                for h in range(2)
            ]
        with jax.named_scope("f_place"):
            for v in range(VIEWS):
                for part in range(2):
                    halves = []
                    for h in range(2):
                        offset = shift[s, v, h]
                        rows = [
                            sums[h][v * WIN + 8 * i : v * WIN + 8 * i + 8, 128 * part : 128 * part + 128]
                            for i in range(WIN // 8)
                        ] + [None] * (32 - WIN // 8)
                        for bit in (8, 16, 32, 64, 128):
                            moved = (offset & bit) != 0
                            step = bit // 8
                            new = []
                            for i in range(32):
                                old, other = rows[i], rows[(i - step) % 32]
                                if old is None and other is None:
                                    new.append(None)
                                elif old is None:
                                    new.append(jnp.where(moved, other, 0.0))
                                elif other is None:
                                    new.append(jnp.where(moved, 0.0, old))
                                else:
                                    new.append(jnp.where(moved, other, old))
                            rows = new
                        halves.append(rows)
                    for i in range(16):
                        for b in range(2):
                            value = halves[0][16 * b + i] + halves[1][16 * b + i]
                            at = slice(128 * v + 8 * i, 128 * v + 8 * i + 8)
                            high, low = in_two(value)
                            if part == 0:
                                window[at, 384 * b : 384 * b + 128] = high
                                window[at, 384 * b + 128 : 384 * b + 256] = low
                            else:
                                window[at, 384 * b + 256 : 384 * b + 384] = jnp.where(lane % 16 == 0, high, low)
        with jax.named_scope("f_mix"):
            mixed = lax.dot_general(
                mixer[...], window[...].astype(BF16), (((1,), (1,)), ((), ())), preferred_element_type=F32
            )
            count = 16 * KINDS
            for v in range(VIEWS):
                for k in range(KINDS):
                    columns = slice(128 * v, 128 * v + 128)
                    send_a[s, k, v] = (
                        mixed[16 * k : 16 * k + 16, columns] + mixed[count + 16 * k : count + 16 * k + 16, columns]
                    )
        with jax.named_scope("f_send"):
            for there, plane, slot, group in ((below, g - 1, 0, GROUPS - 1), (above, g + 1, KINDS - 1, 0)):
                @pl.when(there)
                def _():
                    for v in range(VIEWS):
                        remote(
                            send_a.at[s, slot, v], recv_a.at[s, 1, j], sem_as.at[2 + s], sem_ah.at[s],
                            plane, 2 * (GROUPS * v + group) + 1,
                        )
            to_owners(
                lambda o: send_a.at[s, 1 + lax.rem(o, GROUPS), lax.div(o, GROUPS)],
                recv_a.at[s, 0, j], sem_as.at[s], sem_ar.at[s],
            )

            @pl.when(owner)
            def _():
                recv_a[s, 0, j] = send_a[s, 1 + own_group, own_view]

    def prepare_owner():
        arrived(recv_m.at[0 : xy - 1], sem_mr)
        for block in range(blocks):
            first, last = 128 * block, 128 * block + 128
            for s in range(SUBSETS):
                value = jnp.zeros((8, 128), F32)
                for i in range(first // COLS_DEV, min(xy, -(-last // COLS_DEV))):
                    low, high = max(COLS_DEV * i, first) - first, min(COLS_DEV * (i + 1), last) - first
                    piece = recv_m[i, 8 * s : 8 * s + 8, :]
                    value = jnp.where(jnp.logical_and(lane >= low, lane < high), piece, value)
                meas_rows[s, block] = value

    def window_starts(s):
        cosine, sine = trig[s, own_view, 0], trig[s, own_view, 1]

        def one(i, carry):
            x = jnp.full((8, 128), i * X_DEV, jnp.int32).astype(F32) + ((X_DEV - 1) / 2.0 - (nx_all - 1) / 2.0)
            starts[s, i] = jnp.floor(project(x, 0.0, cosine, sine)) - 128.0
            return carry

        lax.fori_loop(0, xy, one, 0)

    def owner_work(s):
        with jax.named_scope("wait_a"):
            arrived(recv_a.at[s, 0, 0 : xy - 1], sem_ar.at[s])

        def adder(source):
            def add(i, sums):
                start = starts[s, i]
                parts = recv_a[s, source, i, 0:8, :], recv_a[s, source, i, 8:16, :]
                new = []
                for m in range(blocks):
                    away = column_ids[m] - start
                    hit = jnp.logical_and(away >= 0.0, away < 256.0)
                    new.append(sums[m] + jnp.where(hit, parts[m % 2], 0.0))
                return tuple(new)

            return lax.fori_loop(0, xy, add, tuple(jnp.zeros((8, 128), F32) for _ in range(blocks)))

        with jax.named_scope("o_add"):
            sums = adder(0)
            for m in range(blocks):
                total[m] = sums[m]

        @pl.when(has_beside)
        def _():
            with jax.named_scope("wait_h"):
                arrived(recv_a.at[s, 1], sem_ah.at[s])
            with jax.named_scope("o_addh"):
                sums = adder(1)
                for m in range(blocks):
                    total[m] = total[m] + sums[m]

        with jax.named_scope("o_give"):
            residuals = []
            for m in range(blocks):
                value = total[m]
                columns = jnp.broadcast_to(value[7:8, :], (8, 128))
                residual = meas_rows[s, m] - value / jnp.maximum(ray_row * columns, 1.0)
                residual = jnp.where(own_slot, residual, 0.0)
                total[m] = residual
                residuals.append(rounded(residual))

            def give(i, carry):
                start = starts[s, i]
                parts = []
                for b in range(2):
                    message = residuals[blocks - 2 + b]
                    for m in range(blocks - 4 + b, -1, -2):
                        message = jnp.where(column_ids[m] >= start, residuals[m], message)
                    parts.append(message)
                send_c[s, i] = jnp.concatenate(parts, axis=0).astype(BF16)
                return carry

            lax.fori_loop(0, xy, give, 0)

        with jax.named_scope("o_send"):
            @pl.when(give_down)
            def _():
                for t in range(xy):
                    i = next_device(t)
                    remote(
                        send_c.at[s, i], recv_c.at[s, OWNERS + VIEWS + own_view],
                        sem_cs.at[2 + s], sem_ch.at[s, 1], g - 1, i,
                    )

            @pl.when(give_up)
            def _():
                for t in range(xy):
                    i = next_device(t)
                    remote(
                        send_c.at[s, i], recv_c.at[s, OWNERS + own_view], sem_cs.at[2 + s], sem_ch.at[s, 0], g + 1, i
                    )

            for t in range(1, xy):
                i = next_device(t)
                remote(send_c.at[s, i], recv_c.at[s, chip], sem_cs.at[s], sem_cr.at[s], g, i)
            recv_c[s, chip] = send_c[s, j]

    def owner_give_residual():
        for i in range(xy):
            first = COLS_DEV * i // 128
            message = total[first]
            if first + 1 < blocks:
                message = jnp.where(lane >= COLS_DEV * i % 128, message, total[first + 1])
            send_d[i] = message
        for t in range(1, xy):
            i = next_device(t)
            remote(send_d.at[i], recv_d.at[chip], sem_ds, sem_dr, g, i)
        recv_d[chip] = send_d[j]

    def backward(s):
        @pl.when(jnp.logical_not(below))
        def _():
            recv_c[s, OWNERS : OWNERS + VIEWS] = jnp.zeros((VIEWS, 16, 128), BF16)

        @pl.when(jnp.logical_not(above))
        def _():
            recv_c[s, OWNERS + VIEWS : OWNERS + 2 * VIEWS] = jnp.zeros((VIEWS, 16, 128), BF16)

        with jax.named_scope("wait_c"):
            with_owners(recv_c.at[s], sem_cr.at[s])

        with jax.named_scope("wait_ch"):
            @pl.when(below)
            def _():
                arrived(recv_c.at[s, OWNERS : OWNERS + VIEWS], sem_ch.at[s, 0])

            @pl.when(above)
            def _():
                arrived(recv_c.at[s, OWNERS + VIEWS : OWNERS + 2 * VIEWS], sem_ch.at[s, 1])

        with jax.named_scope("b_smear"):
            columns = []
            for v in range(VIEWS):
                from_rows = [OWNERS + v] + [GROUPS * v + k for k in range(GROUPS)] + [OWNERS + VIEWS + v]
                rows = jnp.concatenate(
                    [recv_c[s, at].astype(F32) for at in from_rows] + [jnp.zeros((128 - 16 * KINDS, 128), F32)],
                    axis=0,
                )
                flipped = jnp.transpose(rows).astype(BF16)
                columns.append(jnp.concatenate([flipped, flipped], axis=1))
            smeared = rounded(
                lax.dot_general(
                    jnp.concatenate(columns, axis=0), smearer[...], (((1,), (0,)), ((), ())),
                    preferred_element_type=F32,
                )
            )
            for v in range(VIEWS):
                whole = [
                    smeared[128 * v + 8 * i : 128 * v + 8 * i + 8, 128 * p : 128 * p + 128]
                    for p in range(2)
                    for i in range(16)
                ]
                for h in range(2):
                    offset = shift[s, v, h]
                    now = whole
                    for bit in (128, 64, 32, 16, 8):
                        step = bit // 8
                        moved = (offset & bit) != 0
                        now = [
                            jnp.where(moved, now[(i + step) % 32], now[i]) for i in range(WIN // 8 + step - 1)
                        ]
                    for i in range(WIN // 8):
                        turned[h, v * WIN + 8 * i : v * WIN + 8 * i + 8, :] = now[i]
        with jax.named_scope("b_turn"):
            sides = [jnp.transpose(turned[h]).astype(BF16) for h in range(2)]
        last = s == SUBSETS - 1
        per_step = 4

        def one(step, carry):
            for h in range(2):
                columns = pl.ds(pl.multiple_of(step * (128 * per_step), 128 * per_step), 128 * per_step)
                back = lax.dot_general(
                    sides[h], weights[2 * s + h, :, columns], (((1,), (0,)), ((), ())),
                    preferred_element_type=F32,
                )
                for part in range(per_step):
                    x = per_step * step + part
                    mine = back[112:128, 128 * part : 128 * part + 128]
                    for q in range(6, -1, -1):
                        mine = jnp.where(
                            jnp.concatenate([band, band], axis=0) == q,
                            back[16 * q : 16 * q + 16, 128 * part : 128 * part + 128], mine,
                        )
                    norm = slice_total * ws[s, pl.ds(HALF * h + x, 1), :]
                    at = pl.ds(HALF * h + x, 16, stride=X_DEV)
                    new = it[at, :] + mine / jnp.maximum(norm, 1.0)
                    if last:
                        out_ref[at, :] = new
                    else:
                        it[at, :] = new
                        spread(new, h, x)
            return carry

        with jax.named_scope("b_loop"):
            lax.fori_loop(0, HALF // per_step, one, 0)

    with jax.named_scope("send_m"):
        send_measured()
    forward(0)

    @pl.when(owner)
    def _():
        with jax.named_scope("prep"):
            prepare_owner()
            window_starts(0)
        owner_work(0)

    with jax.named_scope("gw1"):
        geometry(1)
        make_weights(1)

    @pl.when(owner)
    def _():
        window_starts(1)

    backward(0)
    forward(1)

    @pl.when(owner)
    def _():
        owner_work(1)
        with jax.named_scope("give"):
            owner_give_residual()

    backward(1)

    with jax.named_scope("tail"):
        with_owners(recv_d, sem_dr)
        turn_back = lax.rem(128 - lax.rem(j * COLS_DEV, 128), 128)
        for v in range(VIEWS):
            for k in range(GROUPS):
                message = pltpu.roll(recv_d[GROUPS * v + k], turn_back, 1)
                resid_ref[v, SLOTS * k : SLOTS * k + SIZES[k], :] = message[0 : SIZES[k], 0:COLS_DEV]

        with_owners(send_m, sem_ms)
        for s in range(SUBSETS):
            with_owners(recv_a.at[s, 0], sem_as.at[s])

            @pl.when(below)
            def _():
                arrived(send_a.at[s, 0], sem_as.at[2 + s])

            @pl.when(above)
            def _():
                arrived(send_a.at[s, KINDS - 1], sem_as.at[2 + s])

            @pl.when(owner)
            def _():
                arrived(send_c.at[s, 0 : xy - 1], sem_cs.at[s])

                @pl.when(has_beside)
                def _():
                    arrived(send_c.at[s], sem_cs.at[2 + s])

        @pl.when(owner)
        def _():
            arrived(send_d.at[0 : xy - 1], sem_ds)


def local(gz, xy, volume, measured, view_order):
    blocks = COLS_DEV * xy // 128
    dma = pltpu.SemaphoreType.DMA
    vmem = pltpu.VMEM
    out, resid = pl.pallas_call(
        functools.partial(kernel, gz, xy),
        out_shape=(
            jax.ShapeDtypeStruct((Z_DEV * X_DEV, NY), F32),
            jax.ShapeDtypeStruct((VIEWS, ROWS_DEV, COLS_DEV), F32),
        ),
        in_specs=[pl.BlockSpec(memory_space=pl.ANY)] * 3,
        out_specs=(pl.BlockSpec(memory_space=pltpu.VMEM), pl.BlockSpec(memory_space=pltpu.VMEM)),
        scratch_shapes=[
            pltpu.SMEM((ANGLES,), jnp.int32),
            vmem((Z_DEV * X_DEV, NY), F32),
            vmem((VIEWS, ROWS_DEV, SUBSETS, COLS_DEV), F32),
            vmem((SUBSETS, VIEWS, X_DEV, NY), F32),
            vmem((SUBSETS, X_DEV, NY), F32),
            vmem((SUBSETS, VIEWS, 2, 8, 128), jnp.int32),
            vmem((SUBSETS, VIEWS, 2, 8, 128), F32),
            vmem((2 * SUBSETS, VIEWS * WIN, HALF * NY), BF16),
            vmem((2, 256, HALF * NY), BF16),
            vmem((VIEWS * 128, 768), F32),
            vmem((32 * KINDS, 768), BF16),
            vmem((256, 256), BF16),
            vmem((OWNERS, 16, 128), F32),
            vmem((xy, 16, 128), F32),
            vmem((SUBSETS, blocks, 8, 128), F32),
            vmem((SUBSETS, KINDS, VIEWS, 16, 128), F32),
            vmem((SUBSETS, 2, xy, 16, 128), F32),
            vmem((SUBSETS, xy, 8, 128), F32),
            vmem((blocks, 8, 128), F32),
            vmem((SUBSETS, xy, 16, 128), BF16),
            vmem((SUBSETS, OWNERS + 2 * VIEWS, 16, 128), BF16),
            vmem((xy, 8, 128), F32),
            vmem((OWNERS, 8, 128), F32),
            vmem((2, VIEWS * WIN, 128), F32),
            dma(()), dma(()), dma(()), dma(()), dma(()), dma((4,)), dma((2,)), dma((2,)),
            dma((4,)), dma((2,)), dma((2, 2)), dma(()), dma(()),
        ],
        compiler_params=pltpu.CompilerParams(collective_id=0, has_side_effects=True),
    )(view_order, volume.reshape(Z_DEV * X_DEV, NY), measured.transpose(1, 2, 0, 3))
    return out.reshape(Z_DEV, X_DEV, NY), resid


def solution(mesh):
    in_specs = (P("gz", "xy", None), P(None, None, "gz", "xy"), P())
    out_specs = (P("gz", "xy", None), P(None, "gz", "xy"))
    body = functools.partial(local, mesh.shape["gz"], mesh.shape["xy"])
    return jax.shard_map(body, mesh=mesh, in_specs=in_specs, out_specs=out_specs, check_vma=False)
```

time: 56.8 us -> 44.8 us (0.79)
  Pallas kernels: 52 us -> 41.5 us
  local copies, waits for them, and re-layouts: 3.97 us -> 2.41 us
    pallas_call x1, Pallas kernels: 52 us -> 41.5 us  [local(): pl.pallas_call(functools.partial(kernel, gz, xy), out_shape=(jax.ShapeDty...]
    unnamed x5 -> x4, local copies, waits for them, and re-layouts: 3.97 us -> 2.41 us
where the time goes in v1:
time: 44.8 us; the launch traced here: 44.5 us
  Pallas kernels  41.5 us (93%)
  local copies, waits for them, and re-layouts  2.41 us (5%)
  between operations  0.65 us (1%)
    pallas_call x1, Pallas kernels, local(): pl.pallas_call(functools.partial(kernel, gz, xy), out_shape=(jax.ShapeDty...  41.5 us
    unnamed x4, local copies, waits for them, and re-layouts  2.41 us

profile of v1, /device:TPU:33, one launch (start us, length us, event | category | flops | bytes accessed | tf_op | source)
XLA Modules:
  0.0 44.5 jit_solution(6138363659351053584)
XLA Ops:
  0.6 41.5 %shard_map.50 = (f32[768,128]{1,0:T(8,128)}, f32[5,20,48]{2,1,0:T(8,128)}) custom-call(s32[48]{0:T(128)} %view_hbm.1, f32[768,128]{1,0:T(8,128)} %bitcast.3, f32[5,20,2,48]{3,2,1,0:T(2,128)} %bitcast.5), custom_call_target="tpu_custom_call" | custom-call | tf_op jit(solution)/shard_map/pallas_call | solution.py:653
  42.1 0.0 copy-start
  42.1 1.8 %copy.7 = f32[16,48,128]{2,1,0:T(8,128)} copy(f32[16,48,128]{2,1,0:T(8,128)} %bitcast.4) | data formatting | bytes 786432
  43.9 0.0 copy-done
  43.9 0.6 %copy.8 = f32[5,20,48]{2,1,0:T(8,128)} copy(f32[5,20,48]{2,1,0:T(8,128)S(1)} %copy-done) | data formatting | bytes 38400
Async XLA Ops:
  42.1 1.8 %copy-start = (f32[5,20,48]{2,1,0:T(8,128)S(1)}, f32[5,20,48]{2,1,0:T(8,128)}, u32[]{:S(2)}) copy-start(f32[5,20,48]{2,1,0:T(8,128)} %get-tuple-element.9) | copy-start | bytes 57604

commit v2 on v1

--- a/solution.py
+++ b/solution.py
@@ -22,8 +22,9 @@
 SLOTS = 7
 SIZES = (7, 7, 6)
 OWNERS = VIEWS * GROUPS
-MESSAGES = ((-1, GROUPS - 1), (0, 0), (0, 1), (0, 2), (1, 0))
-KINDS = len(MESSAGES)
+EDGE = 4
+EDGE_SLOT = ROWS_DEV - EDGE - SLOTS * (GROUPS - 1)
+ROWS = 16 * GROUPS + 16
 MESH = pl.DeviceIdType.MESH
 F32 = jnp.float32
 BF16 = jnp.bfloat16
@@ -35,8 +36,9 @@
 
 def kernel(
     gz, xy, view_hbm, vol_ref, meas_hbm, out_ref, resid_ref,
-    views, it, meas, up, ws, shift, trig, weights, data, window, mixer, smearer,
-    send_m, recv_m, meas_rows, send_a, recv_a, starts, total, send_c, recv_c, send_d, recv_d, turned,
+    views, it, meas, low_id, low_w, high_w, ws, shift, trig, weights, data, window, counted, counted_ahead, count_rows, mixer, smearer,
+    send_m, recv_m, meas_rows, send_a, recv_a, send_e, recv_e, starts, total, send_c, recv_c, send_f, recv_f,
+    send_d, recv_d, turned,
     sem_view, sem_vol, sem_meas, sem_ms, sem_mr, sem_as, sem_ar, sem_ah, sem_cs, sem_cr, sem_ch, sem_ds, sem_dr,
 ):
     g = lax.axis_index("gz")
@@ -162,24 +164,32 @@
                 x = (x_first + (8.0 * block + sub_f)) - (nx_all - 1) / 2.0
                 y = lane_f - (ny_all - 1) / 2.0
                 u = project(x, y, cosine, sine)
-                up[s, v, 8 * block : 8 * block + 8, :] = u - base[block // (HALF // 8)]
                 low = jnp.floor(u)
-                both = rounded(jnp.maximum(0.0, 1.0 - jnp.abs(u - low))) + rounded(
-                    jnp.maximum(0.0, 1.0 - jnp.abs(u - (low + 1.0)))
-                )
+                first = rounded(jnp.maximum(0.0, 1.0 - jnp.abs(u - low)))
+                second = rounded(jnp.maximum(0.0, 1.0 - jnp.abs(u - (low + 1.0))))
+                both = first + second
                 rows = slice(8 * block, 8 * block + 8)
+                low_id[s, v, rows, :] = low - base[block // (HALF // 8)]
+                low_w[s, v, rows, :] = first
+                high_w[s, v, rows, :] = second
                 ws[s, rows, :] = both if v == 0 else ws[s, rows, :] + both
 
-    window_ids = iota((WIN, 128), 0).astype(F32)
+    window_ids = [(iota((16, 128), 0) + 16 * t).astype(F32).astype(BF16) for t in range(WIN // 16)]
+    window_ids_less = [(iota((16, 128), 0) + (16 * t - 1)).astype(F32).astype(BF16) for t in range(WIN // 16)]
 
     def make_weights(s):
         def one(x, carry):
             columns = pl.ds(pl.multiple_of(x * 128, 128), 128)
             for h in range(2):
                 for v in range(VIEWS):
-                    u = up[s, v, pl.ds(HALF * h + x, 1), :]
-                    w = jnp.maximum(0.0, 1.0 - jnp.abs(u - window_ids))
-                    weights[2 * s + h, v * WIN : (v + 1) * WIN, columns] = w.astype(BF16)
+                    row = pl.ds(HALF * h + x, 1)
+                    at, first, second = (
+                        jnp.broadcast_to(ref[s, v, row, :], (16, 128)).astype(BF16) for ref in (low_id, low_w, high_w)
+                    )
+                    for t in range(WIN // 16):
+                        w = jnp.where(window_ids[t] == at, first, jnp.zeros_like(first))
+                        w = jnp.where(window_ids_less[t] == at, second, w)
+                        weights[2 * s + h, v * WIN + 16 * t : v * WIN + 16 * t + 16, columns] = w
             return carry
 
         lax.fori_loop(0, HALF, one, 0)
@@ -193,30 +203,29 @@
             data[h, 16 * q : 16 * q + 16, columns] = values * band_masks[q]
 
     def row_tables():
-        shape = (128, 128)
+        shape = (ROWS, 128)
         at = iota(shape, 0)
-        kind, half, slot = at // 16, (at // 8) % 2, at % 8
-        row = jnp.where(kind == 0, slot + (SLOTS * MESSAGES[0][1] - ROWS_DEV), SLOTS * (kind - 1) + slot)
-        row = jnp.where(kind == KINDS - 1, slot + ROWS_DEV, row)
-        size = jnp.where(jnp.logical_or(kind == 0, kind == GROUPS), SIZES[-1], SLOTS)
+        own = at < 16 * GROUPS
+        half = jnp.where(own, (at // 8) % 2, (at // 4) % 2)
+        slot = jnp.where(own, at % 8, at % 4)
+        edge = jnp.where(at < 16 * GROUPS + 8, -EDGE, ROWS_DEV)
+        row = slot + jnp.where(own, SLOTS * (at // 16), edge)
+        size = jnp.where(at // 16 == GROUPS - 1, SIZES[-1], SLOTS)
         row_all = g * ROWS_DEV + row
         inside = jnp.logical_and(jnp.logical_and(row_all >= 0, row_all < dr_all), slot < size)
-        inside = jnp.logical_and(inside, kind < KINDS)
         slice_all = (g * Z_DEV + iota(shape, 1) % 16).astype(F32)
         row_hat = jnp.where(inside, hat(row_all.astype(F32), slice_all), 0.0)
-        own = jnp.logical_and(jnp.logical_and(kind >= 1, kind <= GROUPS), slot == 7)
-        counts = jnp.where(jnp.logical_and(own, iota(shape, 1) % 16 < 2), 1.0, 0.0)
-        count = 16 * KINDS
+        counts = jnp.where(jnp.logical_and(jnp.logical_and(own, slot == 7), iota(shape, 1) % 16 < 2), 1.0, 0.0)
         for b in range(2):
             mine = half == b
             high, low = in_two(jnp.where(mine, row_hat, 0.0))
-            ones = jnp.where(mine, counts, 0.0)
-            smearer[0:128, 128 * b : 128 * b + 128] = high.astype(BF16)
-            smearer[128:256, 128 * b : 128 * b + 128] = low.astype(BF16)
-            for part, first, second in ((0, high, low), (1, high, low), (2, ones, jnp.zeros(shape, F32))):
-                columns = slice(384 * b + 128 * part, 384 * b + 128 * part + 128)
-                mixer[0:count, columns] = first[0:count].astype(BF16)
-                mixer[count : 2 * count, columns] = second[0:count].astype(BF16)
+            smearer[0:ROWS, 128 * b : 128 * b + 128] = high.astype(BF16)
+            smearer[ROWS : 2 * ROWS, 128 * b : 128 * b + 128] = low.astype(BF16)
+            for part in range(2):
+                columns = slice(256 * b + 128 * part, 256 * b + 128 * part + 128)
+                mixer[0:ROWS, columns] = high.astype(BF16)
+                mixer[ROWS : 2 * ROWS, columns] = low.astype(BF16)
+            count_rows[:, 128 * b : 128 * b + 128] = jnp.where(mine, counts, 0.0).astype(BF16)
 
     slices = (g * Z_DEV + iota((16, 128), 0)).astype(F32)
     slice_total = jnp.zeros((16, 1), F32)
@@ -312,78 +321,98 @@
         def _():
             recv_m[j] = send_m[chip]
 
-    def forward(s):
+    def placed(sums, s, v, part):
+        halves = []
+        for h in range(2):
+            offset = shift[s, v, h]
+            rows = [
+                sums[h][v * WIN + 8 * i : v * WIN + 8 * i + 8, 128 * part : 128 * part + 128] for i in range(WIN // 8)
+            ] + [None] * (32 - WIN // 8)
+            for bit in (8, 16, 32, 64, 128):
+                moved = (offset & bit) != 0
+                step = bit // 8
+                new = []
+                for i in range(32):
+                    old, other = rows[i], rows[(i - step) % 32]
+                    if old is None and other is None:
+                        new.append(None)
+                    elif old is None:
+                        new.append(jnp.where(moved, other, 0.0))
+                    elif other is None:
+                        new.append(jnp.where(moved, 0.0, old))
+                    else:
+                        new.append(jnp.where(moved, other, old))
+                rows = new
+            halves.append(rows)
+        return [a + b for a, b in zip(*halves)]
+
+    def pairs(pieces):
+        for i in range(0, 32, 2):
+            yield i // 16, 8 * (i % 16), jnp.concatenate([pieces[i], pieces[i + 1]], axis=0)
+
+    def band_sums(s, part):
+        rows = slice(0, 256) if part is None else slice(128 * part, 128 * part + 128)
+        return [
+            lax.dot_general(
+                weights[2 * s + h], data[h, rows, :], (((1,), (1,)), ((), ())), preferred_element_type=F32
+            )
+            for h in range(2)
+        ]
+
+    first_lane = iota((16, 128), 1) % 16 == 0
+
+    def count_columns(s, sums, part):
+        for v in range(VIEWS):
+            for b, at, value in pairs(placed(sums, s, v, part)):
+                high, low = in_two(value)
+                counted[128 * v + at : 128 * v + at + 16, 128 * b : 128 * b + 128] = jnp.where(
+                    first_lane, high, low
+                ).astype(BF16)
+        return lax.dot_general(
+            count_rows[...], counted[...], (((1,), (1,)), ((), ())), preferred_element_type=F32
+        )
+
+    def forward(s, counts):
         with jax.named_scope("f_dot"):
-            sums = [
-                lax.dot_general(
-                    weights[2 * s + h], data[h], (((1,), (1,)), ((), ())), preferred_element_type=F32
-                )
-                for h in range(2)
-            ]
+            sums = band_sums(s, None if counts is None else 0)
         with jax.named_scope("f_place"):
             for v in range(VIEWS):
-                for part in range(2):
-                    halves = []
-                    for h in range(2):
-                        offset = shift[s, v, h]
-                        rows = [
-                            sums[h][v * WIN + 8 * i : v * WIN + 8 * i + 8, 128 * part : 128 * part + 128]
-                            for i in range(WIN // 8)
-                        ] + [None] * (32 - WIN // 8)
-                        for bit in (8, 16, 32, 64, 128):
-                            moved = (offset & bit) != 0
-                            step = bit // 8
-                            new = []
-                            for i in range(32):
-                                old, other = rows[i], rows[(i - step) % 32]
-                                if old is None and other is None:
-                                    new.append(None)
-                                elif old is None:
-                                    new.append(jnp.where(moved, other, 0.0))
-                                elif other is None:
-                                    new.append(jnp.where(moved, 0.0, old))
-                                else:
-                                    new.append(jnp.where(moved, other, old))
-                            rows = new
-                        halves.append(rows)
-                    for i in range(16):
-                        for b in range(2):
-                            value = halves[0][16 * b + i] + halves[1][16 * b + i]
-                            at = slice(128 * v + 8 * i, 128 * v + 8 * i + 8)
-                            high, low = in_two(value)
-                            if part == 0:
-                                window[at, 384 * b : 384 * b + 128] = high
-                                window[at, 384 * b + 128 : 384 * b + 256] = low
-                            else:
-                                window[at, 384 * b + 256 : 384 * b + 384] = jnp.where(lane % 16 == 0, high, low)
+                for b, at, value in pairs(placed(sums, s, v, 0)):
+                    high, low = in_two(value)
+                    rows = slice(128 * v + at, 128 * v + at + 16)
+                    window[rows, 256 * b : 256 * b + 128] = high.astype(BF16)
+                    window[rows, 256 * b + 128 : 256 * b + 256] = low.astype(BF16)
         with jax.named_scope("f_mix"):
+            if counts is None:
+                counts = count_columns(s, sums, 1)
             mixed = lax.dot_general(
-                mixer[...], window[...].astype(BF16), (((1,), (1,)), ((), ())), preferred_element_type=F32
+                mixer[...], window[...], (((1,), (1,)), ((), ())), preferred_element_type=F32
             )
-            count = 16 * KINDS
+            mixed = mixed[0:ROWS] + mixed[ROWS : 2 * ROWS] + counts
             for v in range(VIEWS):
-                for k in range(KINDS):
-                    columns = slice(128 * v, 128 * v + 128)
-                    send_a[s, k, v] = (
-                        mixed[16 * k : 16 * k + 16, columns] + mixed[count + 16 * k : count + 16 * k + 16, columns]
-                    )
+                columns = slice(128 * v, 128 * v + 128)
+                for k in range(GROUPS):
+                    send_a[s, k, v] = mixed[16 * k : 16 * k + 16, columns]
+                for e in range(2):
+                    at = 16 * GROUPS + 8 * e
+                    send_e[s, e, v] = mixed[at : at + 8, columns]
         with jax.named_scope("f_send"):
-            for there, plane, slot, group in ((below, g - 1, 0, GROUPS - 1), (above, g + 1, KINDS - 1, 0)):
+            for there, plane, e, group in ((below, g - 1, 0, GROUPS - 1), (above, g + 1, 1, 0)):
                 @pl.when(there)
                 def _():
                     for v in range(VIEWS):
                         remote(
-                            send_a.at[s, slot, v], recv_a.at[s, 1, j], sem_as.at[2 + s], sem_ah.at[s],
+                            send_e.at[s, e, v], recv_e.at[s, j], sem_as.at[2 + s], sem_ah.at[s],
                             plane, 2 * (GROUPS * v + group) + 1,
                         )
             to_owners(
-                lambda o: send_a.at[s, 1 + lax.rem(o, GROUPS), lax.div(o, GROUPS)],
-                recv_a.at[s, 0, j], sem_as.at[s], sem_ar.at[s],
+                lambda o: send_a.at[s, lax.rem(o, GROUPS), lax.div(o, GROUPS)],
+                recv_a.at[s, j], sem_as.at[s], sem_ar.at[s],
             )
 
             @pl.when(owner)
             def _():
-                recv_a[s, 0, j] = send_a[s, 1 + own_group, own_view]
+                recv_a[s, j] = send_a[s, own_group, own_view]
 
     def prepare_owner():
         arrived(recv_m.at[0 : xy - 1], sem_mr)
@@ -407,36 +436,52 @@
 
         lax.fori_loop(0, xy, one, 0)
 
+    def reach(i):
+        far = max(abs(X_DEV * i - (nx_all - 1) / 2.0), abs(X_DEV * i + X_DEV - 1 - (nx_all - 1) / 2.0))
+        radius = math.hypot(far, (ny_all - 1) / 2.0)
+        span = scale * radius / math.sqrt(1.0 - (radius / source) ** 2) + 2.0
+        return max(0, int((middle - span) // 128)), min(blocks - 1, int((middle + span) // 128))
+
+    edge_ids = [(256 * m + 128 * (sub // EDGE) + lane).astype(F32) for m in range(blocks // 2)]
+    edge_slot = jnp.where(last_group, EDGE_SLOT, 0)
+
+    def within(ids, start):
+        return jnp.abs(ids - (start + 127.5)) < 128.0
+
+    def choose(ids, values, candidates, start):
+        message = None
+        for m in reversed(candidates):
+            message = values[m] if message is None else jnp.where(ids[m] >= start, values[m], message)
+        return jnp.zeros((8, 128), F32) if message is None else message
+
     def owner_work(s):
         with jax.named_scope("wait_a"):
-            arrived(recv_a.at[s, 0, 0 : xy - 1], sem_ar.at[s])
-
-        def adder(source):
-            def add(i, sums):
+            arrived(recv_a.at[s, 0 : xy - 1], sem_ar.at[s])
+        with jax.named_scope("o_add"):
+            sums = [jnp.zeros((8, 128), F32)] * blocks
+            for i in range(xy):
                 start = starts[s, i]
-                parts = recv_a[s, source, i, 0:8, :], recv_a[s, source, i, 8:16, :]
-                new = []
-                for m in range(blocks):
-                    away = column_ids[m] - start
-                    hit = jnp.logical_and(away >= 0.0, away < 256.0)
-                    new.append(sums[m] + jnp.where(hit, parts[m % 2], 0.0))
-                return tuple(new)
-
-            return lax.fori_loop(0, xy, add, tuple(jnp.zeros((8, 128), F32) for _ in range(blocks)))
-
-        with jax.named_scope("o_add"):
-            sums = adder(0)
+                parts = recv_a[s, i, 0:8, :], recv_a[s, i, 8:16, :]
+                for m in range(reach(i)[0], reach(i)[1] + 1):
+                    sums[m] = sums[m] + jnp.where(within(column_ids[m], start), parts[m % 2], 0.0)
             for m in range(blocks):
                 total[m] = sums[m]
 
         @pl.when(has_beside)
         def _():
             with jax.named_scope("wait_h"):
-                arrived(recv_a.at[s, 1], sem_ah.at[s])
+                arrived(recv_e.at[s], sem_ah.at[s])
             with jax.named_scope("o_addh"):
-                sums = adder(1)
-                for m in range(blocks):
-                    total[m] = total[m] + sums[m]
+                sums = [jnp.zeros((8, 128), F32)] * (blocks // 2)
+                for i in range(xy):
+                    start = starts[s, i]
+                    message = recv_e[s, i]
+                    for m in range(reach(i)[0] // 2, reach(i)[1] // 2 + 1):
+                        sums[m] = sums[m] + jnp.where(within(edge_ids[m], start), message, 0.0)
+                for m in range(blocks // 2):
+                    low = jnp.where(sub < EDGE, sums[m], 0.0)
+                    total[2 * m] = total[2 * m] + pltpu.roll(low, edge_slot, 0)
+                    total[2 * m + 1] = total[2 * m + 1] + pltpu.roll(sums[m] - low, edge_slot + EDGE, 0)
 
         with jax.named_scope("o_give"):
             residuals = []
@@ -447,42 +492,43 @@
                 residual = jnp.where(own_slot, residual, 0.0)
                 total[m] = residual
                 residuals.append(rounded(residual))
-
-            def give(i, carry):
+            for i in range(xy):
                 start = starts[s, i]
                 parts = []
                 for b in range(2):
-                    message = residuals[blocks - 2 + b]
-                    for m in range(blocks - 4 + b, -1, -2):
-                        message = jnp.where(column_ids[m] >= start, residuals[m], message)
-                    parts.append(message)
+                    candidates = [m for m in range(reach(i)[0], reach(i)[1] + 1) if m % 2 == b]
+                    parts.append(choose(column_ids, residuals, candidates, start))
                 send_c[s, i] = jnp.concatenate(parts, axis=0).astype(BF16)
-                return carry
-
-            lax.fori_loop(0, xy, give, 0)
 
         with jax.named_scope("o_send"):
-            @pl.when(give_down)
-            def _():
-                for t in range(xy):
-                    i = next_device(t)
-                    remote(
-                        send_c.at[s, i], recv_c.at[s, OWNERS + VIEWS + own_view],
-                        sem_cs.at[2 + s], sem_ch.at[s, 1], g - 1, i,
-                    )
-
-            @pl.when(give_up)
-            def _():
-                for t in range(xy):
-                    i = next_device(t)
-                    remote(
-                        send_c.at[s, i], recv_c.at[s, OWNERS + own_view], sem_cs.at[2 + s], sem_ch.at[s, 0], g + 1, i
-                    )
-
             for t in range(1, xy):
                 i = next_device(t)
                 remote(send_c.at[s, i], recv_c.at[s, chip], sem_cs.at[s], sem_cr.at[s], g, i)
             recv_c[s, chip] = send_c[s, j]
+
+        @pl.when(has_beside)
+        def _():
+            with jax.named_scope("o_giveh"):
+                back = lax.rem(8 - edge_slot, 8)
+                edges = [
+                    jnp.where(
+                        sub < EDGE,
+                        pltpu.roll(rounded(total[2 * m]), back, 0),
+                        pltpu.roll(rounded(total[2 * m + 1]), lax.rem(back + EDGE, 8), 0),
+                    )
+                    for m in range(blocks // 2)
+                ]
+                for i in range(xy):
+                    candidates = list(range(reach(i)[0] // 2, reach(i)[1] // 2 + 1))
+                    send_f[s, i] = choose(edge_ids, edges, candidates, starts[s, i]).astype(BF16)
+            with jax.named_scope("o_sendh"):
+                plane = jnp.where(last_group, g + 1, g - 1)
+                slot = jnp.where(last_group, 0, 1)
+                for t in range(xy):
+                    i = next_device(t)
+                    remote(
+                        send_f.at[s, i], recv_f.at[s, slot, own_view], sem_cs.at[2 + s], sem_ch.at[s, slot], plane, i
+                    )
 
     def owner_give_residual():
         for i in range(xy):
@@ -499,11 +545,11 @@
     def backward(s):
         @pl.when(jnp.logical_not(below))
         def _():
-            recv_c[s, OWNERS : OWNERS + VIEWS] = jnp.zeros((VIEWS, 16, 128), BF16)
+            recv_f[s, 0] = jnp.zeros((VIEWS, 8, 128), BF16)
 
         @pl.when(jnp.logical_not(above))
         def _():
-            recv_c[s, OWNERS + VIEWS : OWNERS + 2 * VIEWS] = jnp.zeros((VIEWS, 16, 128), BF16)
+            recv_f[s, 1] = jnp.zeros((VIEWS, 8, 128), BF16)
 
         with jax.named_scope("wait_c"):
             with_owners(recv_c.at[s], sem_cr.at[s])
@@ -511,22 +557,18 @@
         with jax.named_scope("wait_ch"):
             @pl.when(below)
             def _():
-                arrived(recv_c.at[s, OWNERS : OWNERS + VIEWS], sem_ch.at[s, 0])
+                arrived(recv_f.at[s, 0], sem_ch.at[s, 0])
 
             @pl.when(above)
             def _():
-                arrived(recv_c.at[s, OWNERS + VIEWS : OWNERS + 2 * VIEWS], sem_ch.at[s, 1])
+                arrived(recv_f.at[s, 1], sem_ch.at[s, 1])
 
         with jax.named_scope("b_smear"):
             columns = []
             for v in range(VIEWS):
-                from_rows = [OWNERS + v] + [GROUPS * v + k for k in range(GROUPS)] + [OWNERS + VIEWS + v]
-                rows = jnp.concatenate(
-                    [recv_c[s, at].astype(F32) for at in from_rows] + [jnp.zeros((128 - 16 * KINDS, 128), F32)],
-                    axis=0,
-                )
-                flipped = jnp.transpose(rows).astype(BF16)
-                columns.append(jnp.concatenate([flipped, flipped], axis=1))
+                rows = [recv_c[s, GROUPS * v + k].astype(F32) for k in range(GROUPS)]
+                rows = rows + [recv_f[s, e, v].astype(F32) for e in range(2)]
+                columns.append(jnp.transpose(jnp.concatenate(rows + rows, axis=0)).astype(BF16))
             smeared = rounded(
                 lax.dot_general(
                     jnp.concatenate(columns, axis=0), smearer[...], (((1,), (0,)), ((), ())),
@@ -585,7 +627,7 @@
 
     with jax.named_scope("send_m"):
         send_measured()
-    forward(0)
+    forward(0, None)
 
     @pl.when(owner)
     def _():
@@ -597,13 +639,14 @@
     with jax.named_scope("gw1"):
         geometry(1)
         make_weights(1)
+        counted_ahead[...] = count_columns(1, band_sums(1, 1), 0)
 
     @pl.when(owner)
     def _():
         window_starts(1)
 
     backward(0)
-    forward(1)
+    forward(1, counted_ahead[...])
 
     @pl.when(owner)
     def _():
@@ -623,23 +666,23 @@
 
         with_owners(send_m, sem_ms)
         for s in range(SUBSETS):
-            with_owners(recv_a.at[s, 0], sem_as.at[s])
+            with_owners(recv_a.at[s], sem_as.at[s])
 
             @pl.when(below)
             def _():
-                arrived(send_a.at[s, 0], sem_as.at[2 + s])
+                arrived(send_e.at[s, 0], sem_as.at[2 + s])
 
             @pl.when(above)
             def _():
-                arrived(send_a.at[s, KINDS - 1], sem_as.at[2 + s])
+                arrived(send_e.at[s, 1], sem_as.at[2 + s])
 
             @pl.when(owner)
             def _():
                 arrived(send_c.at[s, 0 : xy - 1], sem_cs.at[s])
 
-                @pl.when(has_beside)
-                def _():
-                    arrived(send_c.at[s], sem_cs.at[2 + s])
+            @pl.when(has_beside)
+            def _():
+                arrived(send_f.at[s], sem_cs.at[2 + s])
 
         @pl.when(owner)
         def _():
@@ -653,8 +696,8 @@
     out, resid = pl.pallas_call(
         functools.partial(kernel, gz, xy),
         out_shape=(
-            jax.ShapeDtypeStruct((Z_DEV * X_DEV, NY), F32),
-            jax.ShapeDtypeStruct((VIEWS, ROWS_DEV, COLS_DEV), F32),
+            pltpu.VMEM((Z_DEV * X_DEV, NY), F32),
+            pltpu.VMEM((VIEWS, ROWS_DEV, COLS_DEV), F32),
         ),
         in_specs=[pl.BlockSpec(memory_space=pl.ANY)] * 3,
         out_specs=(pl.BlockSpec(memory_space=pltpu.VMEM), pl.BlockSpec(memory_space=pltpu.VMEM)),
@@ -663,23 +706,32 @@
             vmem((Z_DEV * X_DEV, NY), F32),
             vmem((VIEWS, ROWS_DEV, SUBSETS, COLS_DEV), F32),
             vmem((SUBSETS, VIEWS, X_DEV, NY), F32),
+            vmem((SUBSETS, VIEWS, X_DEV, NY), F32),
+            vmem((SUBSETS, VIEWS, X_DEV, NY), F32),
             vmem((SUBSETS, X_DEV, NY), F32),
             vmem((SUBSETS, VIEWS, 2, 8, 128), jnp.int32),
             vmem((SUBSETS, VIEWS, 2, 8, 128), F32),
             vmem((2 * SUBSETS, VIEWS * WIN, HALF * NY), BF16),
             vmem((2, 256, HALF * NY), BF16),
-            vmem((VIEWS * 128, 768), F32),
-            vmem((32 * KINDS, 768), BF16),
-            vmem((256, 256), BF16),
+            vmem((VIEWS * 128, 512), BF16),
+            vmem((VIEWS * 128, 256), BF16),
+            vmem((ROWS, VIEWS * 128), F32),
+            vmem((ROWS, 256), BF16),
+            vmem((2 * ROWS, 512), BF16),
+            vmem((2 * ROWS, 256), BF16),
             vmem((OWNERS, 16, 128), F32),
             vmem((xy, 16, 128), F32),
             vmem((SUBSETS, blocks, 8, 128), F32),
-            vmem((SUBSETS, KINDS, VIEWS, 16, 128), F32),
-            vmem((SUBSETS, 2, xy, 16, 128), F32),
+            vmem((SUBSETS, GROUPS, VIEWS, 16, 128), F32),
+            vmem((SUBSETS, xy, 16, 128), F32),
+            vmem((SUBSETS, 2, VIEWS, 8, 128), F32),
+            vmem((SUBSETS, xy, 8, 128), F32),
             vmem((SUBSETS, xy, 8, 128), F32),
             vmem((blocks, 8, 128), F32),
             vmem((SUBSETS, xy, 16, 128), BF16),
-            vmem((SUBSETS, OWNERS + 2 * VIEWS, 16, 128), BF16),
+            vmem((SUBSETS, OWNERS, 16, 128), BF16),
+            vmem((SUBSETS, xy, 8, 128), BF16),
+            vmem((SUBSETS, 2, VIEWS, 8, 128), BF16),
             vmem((xy, 8, 128), F32),
             vmem((OWNERS, 8, 128), F32),
             vmem((2, VIEWS * WIN, 128), F32),

time: 44.8 us -> 39.6 us (0.88)
  Pallas kernels: 41.5 us -> 37.4 us
  local copies, waits for them, and re-layouts: 2.41 us -> 1.37 us
    pallas_call x1, Pallas kernels: 41.5 us -> 37.4 us  [local(): pl.pallas_call(functools.partial(kernel, gz, xy), out_shape=(pltpu.VMEM((...]
    unnamed x4 -> x2, local copies, waits for them, and re-layouts: 2.41 us -> 1.37 us
where the time goes in v2:
time: 39.6 us; the launch traced here: 39.4 us
  Pallas kernels  37.4 us (94%)
  local copies, waits for them, and re-layouts  1.37 us (3%)
  between operations  0.64 us (2%)
    pallas_call x1, Pallas kernels, local(): pl.pallas_call(functools.partial(kernel, gz, xy), out_shape=(pltpu.VMEM((...  37.4 us
    unnamed x2, local copies, waits for them, and re-layouts  1.37 us

profile of v2, /device:TPU:33, one launch (start us, length us, event | category | flops | bytes accessed | tf_op | source)
XLA Modules:
  0.0 39.4 jit_solution(13024706566718561210)
XLA Ops:
  0.6 37.4 %shard_map.50 = (f32[768,128]{1,0:T(8,128)S(1)}, f32[5,20,48]{2,1,0:T(8,128)S(1)}) custom-call(s32[48]{0:T(128)} %view_hbm.1, f32[768,128]{1,0:T(8,128)} %bitcast.4, f32[5,20,2,48]{3,2,1,0:T(2,128)} %bitcast.5), custom_call_target="tpu_custom_call" | custom-call | tf_op jit(solution)/shard_map/pallas_call | solution.py:696
  38.0 0.7 %copy.7 = f32[16,48,128]{2,1,0:T(8,128)} copy(f32[16,48,128]{2,1,0:T(8,128)S(1)} %bitcast.3) | data formatting | bytes 786432
  38.8 0.6 %copy.8 = f32[5,20,48]{2,1,0:T(8,128)} copy(f32[5,20,48]{2,1,0:T(8,128)S(1)} %get-tuple-element.7) | data formatting | bytes 38400

commit v3 on v2

--- a/solution.py
+++ b/solution.py
@@ -22,6 +22,7 @@
 SLOTS = 7
 SIZES = (7, 7, 6)
 OWNERS = VIEWS * GROUPS
+SIDE = 4
 EDGE = 4
 EDGE_SLOT = ROWS_DEV - EDGE - SLOTS * (GROUPS - 1)
 ROWS = 16 * GROUPS + 16
@@ -78,6 +79,17 @@
 
     def next_device(t):
         return lax.rem(j + t, xy)
+
+    steps = sorted(
+        ((a, b, c) for a in range(SIDE) for b in range(SIDE) for c in (1, 0)),
+        key=lambda step: -sum(min(d, SIDE - d) for d in step[:2]),
+    )
+
+    def moved_chip(a, b):
+        return SIDE * lax.rem(lax.div(chip, SIDE) + a, SIDE) + lax.rem(chip + b, SIDE)
+
+    def moved_device(step):
+        return 2 * moved_chip(step[0], step[1]) + lax.rem(j + step[2], 2)
 
     with jax.named_scope("greet"):
         @pl.when(owner)
@@ -179,7 +191,6 @@
 
     def make_weights(s):
         def one(x, carry):
-            columns = pl.ds(pl.multiple_of(x * 128, 128), 128)
             for h in range(2):
                 for v in range(VIEWS):
                     row = pl.ds(HALF * h + x, 1)
@@ -189,7 +200,7 @@
                     for t in range(WIN // 16):
                         w = jnp.where(window_ids[t] == at, first, jnp.zeros_like(first))
                         w = jnp.where(window_ids_less[t] == at, second, w)
-                        weights[2 * s + h, v * WIN + 16 * t : v * WIN + 16 * t + 16, columns] = w
+                        weights[2 * s + h, x, v * WIN + 16 * t : v * WIN + 16 * t + 16, :] = w
             return carry
 
         lax.fori_loop(0, HALF, one, 0)
@@ -197,10 +208,9 @@
     band_masks = [(iota((16, 128), 1) // 16 == q).astype(F32).astype(BF16) for q in range(8)]
 
     def spread(values, h, x):
-        columns = pl.ds(pl.multiple_of(x * 128, 128), 128)
         values = values.astype(BF16)
         for q in range(8):
-            data[h, 16 * q : 16 * q + 16, columns] = values * band_masks[q]
+            data[h, x, 16 * q : 16 * q + 16, :] = values * band_masks[q]
 
     def row_tables():
         shape = (ROWS, 128)
@@ -254,14 +264,16 @@
         pltpu.make_async_copy(ref, ref, sem).wait()
 
     def to_owners(src, dst, send_sem, recv_sem):
-        for t in range(1, OWNERS):
-            device = next_owner(t)
-            remote(src(lax.div(device, 2)), dst, send_sem, recv_sem, g, device)
-
-        @pl.when(jnp.logical_not(owner))
-        def _():
-            device = next_owner(0)
-            remote(src(lax.div(device, 2)), dst, send_sem, recv_sem, g, device)
+        for a, b, c in steps:
+            if c:
+                there = moved_chip(a, b)
+                wanted = there < OWNERS
+                if a == b == 0:
+                    wanted = jnp.logical_and(wanted, jnp.logical_not(owner))
+
+                @pl.when(wanted)
+                def _():
+                    remote(src(there), dst, send_sem, recv_sem, g, 2 * there + 1)
 
     def with_owners(ref, sem):
         @pl.when(owner)
@@ -273,12 +285,11 @@
             arrived(ref.at[0:OWNERS], sem)
 
     def table(x, carry):
-        columns = pl.ds(pl.multiple_of(x * 128, 128), 128)
         for h in range(2):
             for q in range(8):
                 pair = iota((16, 128), 0) < 2
                 row = jnp.where(jnp.logical_and(pair, iota((16, 128), 1) // 16 == q), 1.0, 0.0)
-                data[h, 128 + 16 * q : 128 + 16 * q + 16, columns] = row.astype(BF16)
+                data[h, x, 128 + 16 * q : 128 + 16 * q + 16, :] = row.astype(BF16)
         return carry
 
     def fill_data(x, carry):
@@ -350,11 +361,15 @@
         for i in range(0, 32, 2):
             yield i // 16, 8 * (i % 16), jnp.concatenate([pieces[i], pieces[i + 1]], axis=0)
 
+    def beside(ref, at, first, count, rows=slice(None)):
+        return jnp.concatenate([ref[at, x, rows, :] for x in range(first, first + count)], axis=1)
+
     def band_sums(s, part):
         rows = slice(0, 256) if part is None else slice(128 * part, 128 * part + 128)
         return [
             lax.dot_general(
-                weights[2 * s + h], data[h, rows, :], (((1,), (1,)), ((), ())), preferred_element_type=F32
+                beside(weights, 2 * s + h, 0, HALF), beside(data, h, 0, HALF, rows),
+                (((1,), (1,)), ((), ())), preferred_element_type=F32,
             )
             for h in range(2)
         ]
@@ -500,12 +515,6 @@
                     parts.append(choose(column_ids, residuals, candidates, start))
                 send_c[s, i] = jnp.concatenate(parts, axis=0).astype(BF16)
 
-        with jax.named_scope("o_send"):
-            for t in range(1, xy):
-                i = next_device(t)
-                remote(send_c.at[s, i], recv_c.at[s, chip], sem_cs.at[s], sem_cr.at[s], g, i)
-            recv_c[s, chip] = send_c[s, j]
-
         @pl.when(has_beside)
         def _():
             with jax.named_scope("o_giveh"):
@@ -524,11 +533,19 @@
             with jax.named_scope("o_sendh"):
                 plane = jnp.where(last_group, g + 1, g - 1)
                 slot = jnp.where(last_group, 0, 1)
-                for t in range(xy):
-                    i = next_device(t)
+                for step in steps:
+                    i = moved_device(step)
                     remote(
                         send_f.at[s, i], recv_f.at[s, slot, own_view], sem_cs.at[2 + s], sem_ch.at[s, slot], plane, i
                     )
+
+        with jax.named_scope("o_send"):
+            for step in steps:
+                if step == (0, 0, 0):
+                    continue
+                i = moved_device(step)
+                remote(send_c.at[s, i], recv_c.at[s, chip], sem_cs.at[s], sem_cr.at[s], g, i)
+            recv_c[s, chip] = send_c[s, j]
 
     def owner_give_residual():
         for i in range(xy):
@@ -595,13 +612,14 @@
         with jax.named_scope("b_turn"):
             sides = [jnp.transpose(turned[h]).astype(BF16) for h in range(2)]
         last = s == SUBSETS - 1
-        per_step = 4
-
-        def one(step, carry):
+        per_step = 2
+
+        bands = jnp.concatenate([band, band], axis=0)
+
+        def one(step):
             for h in range(2):
-                columns = pl.ds(pl.multiple_of(step * (128 * per_step), 128 * per_step), 128 * per_step)
                 back = lax.dot_general(
-                    sides[h], weights[2 * s + h, :, columns], (((1,), (0,)), ((), ())),
+                    sides[h], beside(weights, 2 * s + h, per_step * step, per_step), (((1,), (0,)), ((), ())),
                     preferred_element_type=F32,
                 )
                 for part in range(per_step):
@@ -609,10 +627,9 @@
                     mine = back[112:128, 128 * part : 128 * part + 128]
                     for q in range(6, -1, -1):
                         mine = jnp.where(
-                            jnp.concatenate([band, band], axis=0) == q,
-                            back[16 * q : 16 * q + 16, 128 * part : 128 * part + 128], mine,
+                            bands == q, back[16 * q : 16 * q + 16, 128 * part : 128 * part + 128], mine
                         )
-                    norm = slice_total * ws[s, pl.ds(HALF * h + x, 1), :]
+                    norm = slice_total * ws[s, HALF * h + x : HALF * h + x + 1, :]
                     at = pl.ds(HALF * h + x, 16, stride=X_DEV)
                     new = it[at, :] + mine / jnp.maximum(norm, 1.0)
                     if last:
@@ -620,10 +637,10 @@
                     else:
                         it[at, :] = new
                         spread(new, h, x)
-            return carry
 
         with jax.named_scope("b_loop"):
-            lax.fori_loop(0, HALF // per_step, one, 0)
+            for step in range(HALF // per_step):
+                one(step)
 
     with jax.named_scope("send_m"):
         send_measured()
@@ -711,8 +728,8 @@
             vmem((SUBSETS, X_DEV, NY), F32),
             vmem((SUBSETS, VIEWS, 2, 8, 128), jnp.int32),
             vmem((SUBSETS, VIEWS, 2, 8, 128), F32),
-            vmem((2 * SUBSETS, VIEWS * WIN, HALF * NY), BF16),
-            vmem((2, 256, HALF * NY), BF16),
+            vmem((2 * SUBSETS, HALF, VIEWS * WIN, NY), BF16),
+            vmem((2, HALF, 256, NY), BF16),
             vmem((VIEWS * 128, 512), BF16),
             vmem((VIEWS * 128, 256), BF16),
             vmem((ROWS, VIEWS * 128), F32),

time: 39.6 us -> 36.5 us (0.922)
  Pallas kernels: 37.4 us -> 34.2 us
    pallas_call x1, Pallas kernels: 37.4 us -> 34.2 us  [local(): pl.pallas_call(functools.partial(kernel, gz, xy), out_shape=(pltpu.VMEM((...]
where the time goes in v3:
time: 36.5 us; the launch traced here: 36.2 us
  Pallas kernels  34.2 us (94%)
  local copies, waits for them, and re-layouts  1.37 us (4%)
  between operations  0.64 us (2%)
    pallas_call x1, Pallas kernels, local(): pl.pallas_call(functools.partial(kernel, gz, xy), out_shape=(pltpu.VMEM((...  34.2 us
    unnamed x2, local copies, waits for them, and re-layouts  1.37 us

profile of v3, /device:TPU:33, one launch (start us, length us, event | category | flops | bytes accessed | tf_op | source)
XLA Modules:
  0.0 36.2 jit_solution(2979555215956499534)
XLA Ops:
  0.6 34.2 %shard_map.50 = (f32[768,128]{1,0:T(8,128)S(1)}, f32[5,20,48]{2,1,0:T(8,128)S(1)}) custom-call(s32[48]{0:T(128)} %view_hbm.1, f32[768,128]{1,0:T(8,128)} %bitcast.4, f32[5,20,2,48]{3,2,1,0:T(2,128)} %bitcast.5), custom_call_target="tpu_custom_call" | custom-call | tf_op jit(solution)/shard_map/pallas_call | solution.py:713
  34.9 0.7 %copy.7 = f32[16,48,128]{2,1,0:T(8,128)} copy(f32[16,48,128]{2,1,0:T(8,128)S(1)} %bitcast.3) | data formatting | bytes 786432
  35.6 0.6 %copy.8 = f32[5,20,48]{2,1,0:T(8,128)} copy(f32[5,20,48]{2,1,0:T(8,128)S(1)} %get-tuple-element.7) | data formatting | bytes 38400

commit v4 on v3

--- a/solution.py
+++ b/solution.py
@@ -17,7 +17,8 @@
 ANGLES = 48
 ROWS_DEV = 20
 HALF = X_DEV // 2
-WIN = 48
+WIN = 40
+DEEP = 208
 GROUPS = 3
 SLOTS = 7
 SIZES = (7, 7, 6)
@@ -37,7 +38,7 @@
 
 def kernel(
     gz, xy, view_hbm, vol_ref, meas_hbm, out_ref, resid_ref,
-    views, it, meas, low_id, low_w, high_w, ws, shift, trig, weights, data, window, counted, counted_ahead, count_rows, mixer, smearer,
+    views, it, meas, up, ws, shift, trig, weights, data, window, counted, counted_ahead, count_rows, mixer, smearer,
     send_m, recv_m, meas_rows, send_a, recv_a, send_e, recv_e, starts, total, send_c, recv_c, send_f, recv_f,
     send_d, recv_d, turned,
     sem_view, sem_vol, sem_meas, sem_ms, sem_mr, sem_as, sem_ar, sem_ah, sem_cs, sem_cr, sem_ch, sem_ds, sem_dr,
@@ -181,38 +182,35 @@
                 second = rounded(jnp.maximum(0.0, 1.0 - jnp.abs(u - (low + 1.0))))
                 both = first + second
                 rows = slice(8 * block, 8 * block + 8)
-                low_id[s, v, rows, :] = low - base[block // (HALF // 8)]
-                low_w[s, v, rows, :] = first
-                high_w[s, v, rows, :] = second
+                up[s, v, rows, :] = u - base[block // (HALF // 8)]
                 ws[s, rows, :] = both if v == 0 else ws[s, rows, :] + both
 
-    window_ids = [(iota((16, 128), 0) + 16 * t).astype(F32).astype(BF16) for t in range(WIN // 16)]
-    window_ids_less = [(iota((16, 128), 0) + (16 * t - 1)).astype(F32).astype(BF16) for t in range(WIN // 16)]
+    window_ids = [(sub + 8 * i).astype(F32) for i in range(WIN // 8)]
+
+    def weights_row(s, h, x):
+        pieces = []
+        for v in range(VIEWS):
+            u = jnp.broadcast_to(up[s, v, pl.ds(HALF * h + x, 1), :], (8, 128))
+            pieces += [jnp.maximum(0.0, 1.0 - jnp.abs(u - ids)) for ids in window_ids]
+        pieces.append(jnp.zeros((DEEP - VIEWS * WIN, 128), F32))
+        weights[2 * s + h, x] = jnp.concatenate(pieces, axis=0).astype(BF16)
 
     def make_weights(s):
         def one(x, carry):
             for h in range(2):
-                for v in range(VIEWS):
-                    row = pl.ds(HALF * h + x, 1)
-                    at, first, second = (
-                        jnp.broadcast_to(ref[s, v, row, :], (16, 128)).astype(BF16) for ref in (low_id, low_w, high_w)
-                    )
-                    for t in range(WIN // 16):
-                        w = jnp.where(window_ids[t] == at, first, jnp.zeros_like(first))
-                        w = jnp.where(window_ids_less[t] == at, second, w)
-                        weights[2 * s + h, x, v * WIN + 16 * t : v * WIN + 16 * t + 16, :] = w
+                weights_row(s, h, x)
             return carry
 
-        lax.fori_loop(0, HALF, one, 0)
-
-    band_masks = [(iota((16, 128), 1) // 16 == q).astype(F32).astype(BF16) for q in range(8)]
+        lax.fori_loop(0, HALF, one, 0, unroll=4)
+
+    in_band = [iota((16, 128), 1) // 16 == q for q in range(8)]
 
     def spread(values, h, x):
-        values = values.astype(BF16)
-        for q in range(8):
-            data[h, x, 16 * q : 16 * q + 16, :] = values * band_masks[q]
+        data[h, x, 0:128, :] = jnp.concatenate([jnp.where(mine, values, 0.0) for mine in in_band], axis=0).astype(BF16)
 
     def row_tables():
+        for h in range(2):
+            turned[h, VIEWS * WIN : DEEP, :] = jnp.zeros((DEEP - VIEWS * WIN, 128), F32)
         shape = (ROWS, 128)
         at = iota(shape, 0)
         own = at < 16 * GROUPS
@@ -292,22 +290,23 @@
                 data[h, x, 128 + 16 * q : 128 + 16 * q + 16, :] = row.astype(BF16)
         return carry
 
-    def fill_data(x, carry):
-        for h in range(2):
-            spread(it[pl.ds(HALF * h + x, 16, stride=X_DEV), :], h, x)
+    def spread_row(h, x):
+        spread(it[pl.ds(HALF * h + x, 16, stride=X_DEV), :], h, x)
+
+    def first_half(x, carry):
+        weights_row(0, 0, x)
+        spread_row(0, x)
         return carry
 
+    with jax.named_scope("tables"):
+        row_tables()
+        lax.fori_loop(0, HALF, table, 0, unroll=4)
     view_copy.wait()
     with jax.named_scope("geom0"):
         geometry(0)
-    with jax.named_scope("mw0"):
-        make_weights(0)
-    with jax.named_scope("tables"):
-        row_tables()
-        lax.fori_loop(0, HALF, table, 0)
     with jax.named_scope("fill"):
         vol_copy.wait()
-        lax.fori_loop(0, HALF, fill_data, 0)
+        lax.fori_loop(0, HALF, first_half, 0, unroll=4)
 
     with jax.named_scope("measured"):
         meas_copy.wait()
@@ -364,15 +363,22 @@
     def beside(ref, at, first, count, rows=slice(None)):
         return jnp.concatenate([ref[at, x, rows, :] for x in range(first, first + count)], axis=1)
 
-    def band_sums(s, part):
+    def band_sums(s, part, late=()):
         rows = slice(0, 256) if part is None else slice(128 * part, 128 * part + 128)
-        return [
-            lax.dot_general(
-                beside(weights, 2 * s + h, 0, HALF), beside(data, h, 0, HALF, rows),
-                (((1,), (1,)), ((), ())), preferred_element_type=F32,
+        sums = []
+        for h in range(2):
+            sums.append(
+                lax.dot_general(
+                    beside(weights, 2 * s + h, 0, HALF), beside(data, h, 0, HALF, rows),
+                    (((1,), (1,)), ((), ())), preferred_element_type=F32,
+                )
             )
-            for h in range(2)
-        ]
+            if h == 0:
+                for other in late:
+                    for x in range(HALF):
+                        weights_row(s, other, x)
+                        spread_row(other, x)
+        return sums
 
     first_lane = iota((16, 128), 1) % 16 == 0
 
@@ -389,7 +395,7 @@
 
     def forward(s, counts):
         with jax.named_scope("f_dot"):
-            sums = band_sums(s, None if counts is None else 0)
+            sums = band_sums(s, None, (1,)) if counts is None else band_sums(s, 0)
         with jax.named_scope("f_place"):
             for v in range(VIEWS):
                 for b, at, value in pairs(placed(sums, s, v, 0)):
@@ -616,8 +622,8 @@
 
         bands = jnp.concatenate([band, band], axis=0)
 
-        def one(step):
-            for h in range(2):
+        def one(step, h):
+            if True:
                 back = lax.dot_general(
                     sides[h], beside(weights, 2 * s + h, per_step * step, per_step), (((1,), (0,)), ((), ())),
                     preferred_element_type=F32,
@@ -639,8 +645,9 @@
                         spread(new, h, x)
 
         with jax.named_scope("b_loop"):
-            for step in range(HALF // per_step):
-                one(step)
+            for h in range(2):
+                for step in range(HALF // per_step):
+                    one(step, h)
 
     with jax.named_scope("send_m"):
         send_measured()
@@ -723,12 +730,10 @@
             vmem((Z_DEV * X_DEV, NY), F32),
             vmem((VIEWS, ROWS_DEV, SUBSETS, COLS_DEV), F32),
             vmem((SUBSETS, VIEWS, X_DEV, NY), F32),
-            vmem((SUBSETS, VIEWS, X_DEV, NY), F32),
-            vmem((SUBSETS, VIEWS, X_DEV, NY), F32),
             vmem((SUBSETS, X_DEV, NY), F32),
             vmem((SUBSETS, VIEWS, 2, 8, 128), jnp.int32),
             vmem((SUBSETS, VIEWS, 2, 8, 128), F32),
-            vmem((2 * SUBSETS, HALF, VIEWS * WIN, NY), BF16),
+            vmem((2 * SUBSETS, HALF, DEEP, NY), BF16),
             vmem((2, HALF, 256, NY), BF16),
             vmem((VIEWS * 128, 512), BF16),
             vmem((VIEWS * 128, 256), BF16),
@@ -751,13 +756,31 @@
             vmem((SUBSETS, 2, VIEWS, 8, 128), BF16),
             vmem((xy, 8, 128), F32),
             vmem((OWNERS, 8, 128), F32),
-            vmem((2, VIEWS * WIN, 128), F32),
+            vmem((2, DEEP, 128), F32),
             dma(()), dma(()), dma(()), dma(()), dma(()), dma((4,)), dma((2,)), dma((2,)),
             dma((4,)), dma((2,)), dma((2, 2)), dma(()), dma(()),
         ],
         compiler_params=pltpu.CompilerParams(collective_id=0, has_side_effects=True),
     )(view_order, volume.reshape(Z_DEV * X_DEV, NY), measured.transpose(1, 2, 0, 3))
+    out, resid = pl.pallas_call(
+        put_out,
+        out_shape=(
+            jax.ShapeDtypeStruct((Z_DEV * X_DEV, NY), F32),
+            jax.ShapeDtypeStruct((VIEWS, ROWS_DEV, COLS_DEV), F32),
+        ),
+        in_specs=[pl.BlockSpec(memory_space=pltpu.VMEM)] * 2,
+        out_specs=(pl.BlockSpec(memory_space=pl.ANY),) * 2,
+        scratch_shapes=[dma(()), dma(())],
+    )(pltpu.with_memory_space_constraint(out, pltpu.VMEM), pltpu.with_memory_space_constraint(resid, pltpu.VMEM))
     return out.reshape(Z_DEV, X_DEV, NY), resid
+
+
+def put_out(a_ref, b_ref, a_out, b_out, a_sem, b_sem):
+    copies = [pltpu.make_async_copy(a_ref, a_out, a_sem), pltpu.make_async_copy(b_ref, b_out, b_sem)]
+    for copy in copies:
+        copy.start()
+    for copy in copies:
+        copy.wait()
 
 
 def solution(mesh):

time: 36.5 us -> 36.1 us (0.989)
  local copies, waits for them, and re-layouts: 1.37 us -> 0 us
  Pallas kernels: 34.2 us -> 35.3 us
    unnamed x2 -> x0, local copies, waits for them, and re-layouts: 1.37 us -> none
    pallas_call x0 -> x1, Pallas kernels: none -> 0.77 us  [local(): pl.pallas_call(put_out, out_shape=(jax.ShapeDtypeStruct((Z_DEV * X_DEV, N...]
where the time goes in v4:
time: 36.1 us; the launch traced here: 35.9 us
  Pallas kernels  35.3 us (98%)
  between operations  0.64 us (2%)
    pallas_call x1, Pallas kernels, local(): pl.pallas_call(functools.partial(kernel, gz, xy), out_shape=(pltpu.VMEM((...  34.5 us
    pallas_call x1, Pallas kernels, local(): pl.pallas_call(put_out, out_shape=(jax.ShapeDtypeStruct((Z_DEV * X_DEV, N...  0.77 us

profile of v4, /device:TPU:33, one launch (start us, length us, event | category | flops | bytes accessed | tf_op | source)
XLA Modules:
  0.0 35.9 jit_solution(675127158760096918)
XLA Ops:
  0.6 34.5 %shard_map.50 = (f32[768,128]{1,0:T(8,128)S(1)}, f32[5,20,48]{2,1,0:T(8,128)S(1)}) custom-call(s32[48]{0:T(128)} %view_hbm.1, f32[768,128]{1,0:T(8,128)} %bitcast.3, f32[5,20,2,48]{3,2,1,0:T(2,128)} %bitcast.4), custom_call_target="tpu_custom_call" | custom-call | tf_op jit(solution)/shard_map/pallas_call | solution.py:720
  35.1 0.8 %shard_map.51 = (f32[768,128]{1,0:T(8,128)}, f32[5,20,48]{2,1,0:T(8,128)}) custom-call(f32[768,128]{1,0:T(8,128)S(1)} %get-tuple-element.6.a_ref, f32[5,20,48]{2,1,0:T(8,128)S(1)} %get-tuple-element.7.b_ref), custom_call_target="tpu_custom_call" | custom-call | tf_op jit(solution)/shard_map/pallas_call | solution.py:765

commit v5 on v4

--- a/solution.py
+++ b/solution.py
@@ -321,9 +321,6 @@
         for o in range(OWNERS):
             send_m[o] = pltpu.roll(send_m[o], turn, 1)
 
-    with jax.named_scope("barrier"):
-        pl.semaphore_wait(barrier, greeted)
-
     def send_measured():
         to_owners(lambda o: send_m.at[o], recv_m.at[j], sem_ms, sem_mr)
 
@@ -396,6 +393,11 @@
     def forward(s, counts):
         with jax.named_scope("f_dot"):
             sums = band_sums(s, None, (1,)) if counts is None else band_sums(s, 0)
+        if s == 0:
+            with jax.named_scope("barrier"):
+                pl.semaphore_wait(barrier, greeted)
+            with jax.named_scope("send_m"):
+                send_measured()
         with jax.named_scope("f_place"):
             for v in range(VIEWS):
                 for b, at, value in pairs(placed(sums, s, v, 0)):
@@ -649,8 +651,6 @@
                 for step in range(HALF // per_step):
                     one(step, h)
 
-    with jax.named_scope("send_m"):
-        send_measured()
     forward(0, None)
 
     @pl.when(owner)

time: 36.1 us -> 35.2 us (0.975)
  Pallas kernels: 35.3 us -> 34.5 us
    pallas_call x1, Pallas kernels: 34.5 us -> 33.7 us  [local(): pl.pallas_call(functools.partial(kernel, gz, xy), out_shape=(pltpu.VMEM((...]
where the time goes in v5:
time: 35.2 us; the launch traced here: 35.1 us
  Pallas kernels  34.5 us (98%)
  between operations  0.64 us (2%)
    pallas_call x1, Pallas kernels, local(): pl.pallas_call(functools.partial(kernel, gz, xy), out_shape=(pltpu.VMEM((...  33.7 us
    pallas_call x1, Pallas kernels, local(): pl.pallas_call(put_out, out_shape=(jax.ShapeDtypeStruct((Z_DEV * X_DEV, N...  0.77 us

profile of v5, /device:TPU:33, one launch (start us, length us, event | category | flops | bytes accessed | tf_op | source)
XLA Modules:
  0.0 35.1 jit_solution(1980841383070486307)
XLA Ops:
  0.6 33.7 %shard_map.50 = (f32[768,128]{1,0:T(8,128)S(1)}, f32[5,20,48]{2,1,0:T(8,128)S(1)}) custom-call(s32[48]{0:T(128)} %view_hbm.1, f32[768,128]{1,0:T(8,128)} %bitcast.3, f32[5,20,2,48]{3,2,1,0:T(2,128)} %bitcast.4), custom_call_target="tpu_custom_call" | custom-call | tf_op jit(solution)/shard_map/pallas_call | solution.py:720
  34.3 0.8 %shard_map.51 = (f32[768,128]{1,0:T(8,128)}, f32[5,20,48]{2,1,0:T(8,128)}) custom-call(f32[768,128]{1,0:T(8,128)S(1)} %get-tuple-element.6.a_ref, f32[5,20,48]{2,1,0:T(8,128)S(1)} %get-tuple-element.7.b_ref), custom_call_target="tpu_custom_call" | custom-call | tf_op jit(solution)/shard_map/pallas_call | solution.py:765

commit v6 on v4

--- a/solution.py
+++ b/solution.py
@@ -161,16 +161,14 @@
             trig[s, v, 0] = cosine
             trig[s, v, 1] = sine
             y_low = (band * 16).astype(F32) - (ny_all - 1) / 2.0
+            x = x_first + (HALF * (sub // 4) + (HALF - 1) * ((sub // 2) % 2)).astype(F32) - (nx_all - 1) / 2.0
+            corners = project(x, y_low + (15 * (sub % 2)).astype(F32), cosine, sine)
+            lowest = jnp.minimum(corners, pltpu.roll(corners, 7, 0))
+            lowest = jnp.minimum(lowest, pltpu.roll(lowest, 6, 0))
+            begin = jnp.floor((lowest - 0.03125) * 0.125) * 8.0
             base = []
             for h in range(2):
-                x_low = (x_first + HALF * h) - (nx_all - 1) / 2.0
-                corners = [
-                    project(x, y, cosine, sine)
-                    for x in (x_low, x_low + (HALF - 1))
-                    for y in (y_low, y_low + 15.0)
-                ]
-                lowest = jnp.minimum(jnp.minimum(corners[0], corners[1]), jnp.minimum(corners[2], corners[3]))
-                start = jnp.floor((lowest - 0.03125) * 0.125) * 8.0
+                start = jnp.broadcast_to(begin[4 * h : 4 * h + 1, :], (8, 128))
                 base.append(start)
                 shift[s, v, h] = (start - 256.0 * jnp.floor(start * (1.0 / 256.0))).astype(jnp.int32)
             for block in range(X_DEV // 8):
@@ -321,9 +319,6 @@
         for o in range(OWNERS):
             send_m[o] = pltpu.roll(send_m[o], turn, 1)
 
-    with jax.named_scope("barrier"):
-        pl.semaphore_wait(barrier, greeted)
-
     def send_measured():
         to_owners(lambda o: send_m.at[o], recv_m.at[j], sem_ms, sem_mr)
 
@@ -417,6 +412,11 @@
                 for e in range(2):
                     at = 16 * GROUPS + 8 * e
                     send_e[s, e, v] = mixed[at : at + 8, columns]
+        if s == 0:
+            with jax.named_scope("barrier"):
+                pl.semaphore_wait(barrier, greeted)
+            with jax.named_scope("send_m"):
+                send_measured()
         with jax.named_scope("f_send"):
             for there, plane, e, group in ((below, g - 1, 0, GROUPS - 1), (above, g + 1, 1, 0)):
                 @pl.when(there)
@@ -649,8 +649,6 @@
                 for step in range(HALF // per_step):
                     one(step, h)
 
-    with jax.named_scope("send_m"):
-        send_measured()
     forward(0, None)
 
     @pl.when(owner)

time: 36.1 us -> 35.2 us (0.975)
  Pallas kernels: 35.3 us -> 34.4 us
    pallas_call x1, Pallas kernels: 34.5 us -> 33.7 us  [local(): pl.pallas_call(functools.partial(kernel, gz, xy), out_shape=(pltpu.VMEM((...]
where the time goes in v6:
time: 35.2 us; the launch traced here: 35.1 us
  Pallas kernels  34.4 us (98%)
  between operations  0.64 us (2%)
    pallas_call x1, Pallas kernels, local(): pl.pallas_call(functools.partial(kernel, gz, xy), out_shape=(pltpu.VMEM((...  33.7 us
    pallas_call x1, Pallas kernels, local(): pl.pallas_call(put_out, out_shape=(jax.ShapeDtypeStruct((Z_DEV * X_DEV, N...  0.77 us

profile of v6, /device:TPU:33, one launch (start us, length us, event | category | flops | bytes accessed | tf_op | source)
XLA Modules:
  0.0 35.1 jit_solution(8300133652930874762)
XLA Ops:
  0.6 33.7 %shard_map.50 = (f32[768,128]{1,0:T(8,128)S(1)}, f32[5,20,48]{2,1,0:T(8,128)S(1)}) custom-call(s32[48]{0:T(128)} %view_hbm.1, f32[768,128]{1,0:T(8,128)} %bitcast.3, f32[5,20,2,48]{3,2,1,0:T(2,128)} %bitcast.4), custom_call_target="tpu_custom_call" | custom-call | tf_op jit(solution)/shard_map/pallas_call | solution.py:718
  34.3 0.8 %shard_map.51 = (f32[768,128]{1,0:T(8,128)}, f32[5,20,48]{2,1,0:T(8,128)}) custom-call(f32[768,128]{1,0:T(8,128)S(1)} %get-tuple-element.6.a_ref, f32[5,20,48]{2,1,0:T(8,128)S(1)} %get-tuple-element.7.b_ref), custom_call_target="tpu_custom_call" | custom-call | tf_op jit(solution)/shard_map/pallas_call | solution.py:763
